TPU v7x, 128 devices: a whole 4x4x4 slice. The times are simulated.
128 devices in a mesh: pair: 2 (over core), shard: 64 (over z, y, x).
Axes of the slice: x: 4, y: 4, z: 4, core: 2. Of those that a mesh axis runs over, the one named last changes fastest.
Arguments:
- master: float32 [3072, 4096], P('shard', 'pair'), may hold values from -1.5 to 1.5
- gradient: float32 [3072, 4096], P('shard', 'pair'), may hold values from -40 to 40
- first_moment: float32 [3072, 4096], P('shard', 'pair'), may hold values from -4 to 4
- second_moment: float32 [3072, 4096], P('shard', 'pair'), may hold values from 0.02 to 4
- max_norm: float32 [1], replicated, may hold values from 768 to 1536
- step_count: int32 [1], replicated, may hold values from 1 to 1000
Outputs:
- new_master: float32 [3072, 4096], P('shard', 'pair')
- new_first: float32 [3072, 4096], P('shard', 'pair')
- new_second: float32 [3072, 4096], P('shard', 'pair')
- compute_codes: bfloat16 [3072, 4096], P('pair')
- block_scales: bfloat16 [3072, 128], P('pair')
All inputs are finite; a program needn't handle non-finite values.
Results may differ from a plain program's by a relative error of at most 0.001.
The roundings to bfloat16 on the way count: a program that leaves them out, or rounds other values in their place, can miss the bound.
Values may be sent and summed in bfloat16 or wider, within the bound.
No kernel may reach another device: no remote copies, remote signals or barrier semaphores. Data moves between devices by JAX's collectives and lax.ppermute only.
A program may use at most 192 MiB of HBM per device.

v0:
```python
import functools
import math

import jax
import jax.numpy as jnp
import numpy as np
from jax import lax
from jax.experimental import pallas as pl
from jax.experimental.pallas import tpu as pltpu
from jax.sharding import Mesh
from jax.sharding import PartitionSpec as P


BLOCK = 32
LANES = 128
AXES = ("pair", "shard_0", "shard_1", "shard_2")
SHARD = ("shard_0", "shard_1", "shard_2")
RING = 4

beta_first = 0.9
beta_second = 0.99
learn_rate = 0.01
decay_rate = 0.1
adam_eps = 1e-06
scale_floor = 0.25
log_first = math.log(float(np.float32(beta_first)))
log_second = math.log(float(np.float32(beta_second)))


def everyone():
    for p in range(2):
        for z in range(RING):
            for y in range(RING):
                for x in range(RING):
                    yield p, z, y, x


def flat(p, z, y, x):
    return ((p * RING + z) * RING + y) * RING + x


def near_mask(p):
    return 1 if p == 0 else 3


def far_mask(p):
    return 3 if p == 0 else 1


def squares_kernel(
    max_norm_ref, step_ref, gradient_ref, sums_ref, known_ref
):
    counted = jnp.full((1, LANES), step_ref[0].astype(jnp.float32))
    known_ref[0:1, :] = jnp.full((1, LANES), max_norm_ref[0], jnp.float32)
    known_ref[1:2, :] = 1.0 / (1.0 - jnp.exp(counted * log_first))
    known_ref[2:3, :] = 1.0 / (1.0 - jnp.exp(counted * log_second))
    known_ref[3:, :] = jnp.zeros((known_ref.shape[0] - 3, LANES), jnp.float32)
    rows, cols = gradient_ref.shape
    total = jnp.zeros((rows, LANES), jnp.float32)
    for at in range(0, cols, LANES):
        part = gradient_ref[:, at : at + LANES]
        total = total + part * part
    line = jnp.sum(total, axis=0, keepdims=True)
    sums_ref[...] = jnp.broadcast_to(line, sums_ref.shape)


def adam_kernel(
    sums_ref, known_ref, master_ref, gradient_ref, first_ref, second_ref,
    new_master_ref, new_first_ref, new_second_ref, top_ref, low_ref, one_ref,
):
    rows, cols = master_ref.shape
    line = jnp.sum(sums_ref[...], axis=0, keepdims=True)
    squares = jnp.sum(line, axis=1, keepdims=True)
    norm_limit = known_ref[0:1, :]
    clip_factor = norm_limit / jnp.maximum(jnp.sqrt(squares), norm_limit)
    first_fix = known_ref[1:2, :]
    second_fix = known_ref[2:3, :]

    lane = lax.broadcasted_iota(jnp.int32, (rows, LANES), 1)
    last_of_block = lane % BLOCK == BLOCK - 1
    per = LANES // BLOCK
    at_row = lax.broadcasted_iota(jnp.int32, (LANES, 2 * LANES), 0)
    at_col = lax.broadcasted_iota(jnp.int32, (LANES, 2 * LANES), 1)
    spread = at_row == (at_col // BLOCK) * BLOCK + BLOCK - 1
    gathered = at_row == (at_col % per) * BLOCK + BLOCK - 1
    picks = jnp.where(
        jnp.where(at_col < LANES, spread.astype(jnp.int32), gathered.astype(jnp.int32)) == 1, 1.0, 0.0
    ).astype(jnp.bfloat16)
    group = lane // per - (cols // LANES) * lax.axis_index("pair")

    home = lax.axis_index("pair") == lax.axis_index("shard_0") // 2

    def store(at, values):
        top, low = values[: rows // 2], values[rows // 2 :]
        top_ref[:, at] = top.astype(jnp.bfloat16)
        low_ref[:, at] = low.astype(jnp.bfloat16)
        one_ref[:, at] = jnp.where(home, low, top).astype(jnp.bfloat16)

    scales = jnp.zeros((rows, LANES), jnp.float32)
    for k in range(cols // LANES):
        at = slice(k * LANES, (k + 1) * LANES)
        master = master_ref[:, at]
        clipped = clip_factor * gradient_ref[:, at]
        new_first = beta_first * first_ref[:, at] + (1.0 - beta_first) * clipped
        new_second = beta_second * second_ref[:, at] + (1.0 - beta_second) * clipped * clipped
        update = new_first * first_fix / (jnp.sqrt(new_second * second_fix) + adam_eps) + decay_rate * master
        new_master = master - learn_rate * update
        new_master_ref[:, at] = new_master
        new_first_ref[:, at] = new_first
        new_second_ref[:, at] = new_second
        largest = jnp.abs(new_master)
        for shift in (1, 2, 4, 8, 16):
            largest = jnp.maximum(largest, pltpu.roll(largest, shift, 1))
        kept = jnp.where(last_of_block, jnp.maximum(largest, scale_floor), 0.0).astype(jnp.bfloat16)
        both = jnp.dot(kept, picks, preferred_element_type=jnp.float32)
        store(at, new_master / both[:, :LANES])
        scales = jnp.where(group == k, both[:, LANES:], scales)
    store(slice(cols, cols + LANES), scales)


def join_kernel(top_ref, one_ref, two_ref, out_ref):
    p = lax.axis_index("pair")
    home = lax.axis_index("shard_0") // 2
    cols = top_ref.shape[1] - LANES

    def fill(left, right):
        out_ref[:, :cols] = left[:, :cols]
        out_ref[:, cols : 2 * cols] = right[:, :cols]
        out_ref[:, 2 * cols :] = left[:, cols:] + right[:, cols:]

    pl.when((p == 0) & (home == 0))(lambda: fill(top_ref, one_ref))
    pl.when((p == 1) & (home == 1))(lambda: fill(one_ref, top_ref))
    pl.when((p == 0) & (home == 1))(lambda: fill(one_ref, two_ref))
    pl.when((p == 1) & (home == 0))(lambda: fill(two_ref, one_ref))


def place_kernel(which, *refs):
    pieces, (codes_ref, scales_ref, sem) = refs[: len(which)], refs[-3:]
    p, z, y, x = (lax.axis_index(a) for a in AXES)
    near = 1 + 2 * p
    far = 3 - 2 * p
    wide = codes_ref.shape[-1]
    copies = []
    for piece, (colour, bits) in zip(pieces, which):
        hop = {SHARD[(colour + i) % 3]: (bits >> i) & 1 for i in range(3)}
        for j in range(8):
            zz = z ^ (far * hop[SHARD[0]]) ^ (near * (j & 1))
            yy = y ^ (far * hop[SHARD[1]]) ^ (near * ((j >> 1) & 1))
            xx = x ^ (far * hop[SHARD[2]]) ^ (near * ((j >> 2) & 1))
            away = (zz >> 1) ^ p
            owner = zz ^ (3 * away)
            row = ((owner & 1) * (RING * RING) + yy * RING + xx) * 6 + 3 * away + colour
            copies.append(pltpu.make_async_copy(piece.at[j, :, pl.ds(0, wide)], codes_ref.at[row], sem))
            copies.append(pltpu.make_async_copy(piece.at[j, :, pl.ds(wide, LANES)], scales_ref.at[row], sem))
    for copy in copies:
        copy.start()
    for copy in copies:
        copy.wait()


def permute(value, pairs):
    return lax.ppermute(value, AXES, pairs)


def redistribute(top, low, first):
    one, two = [], []
    for q, z, y, x in everyone():
        if q == z // 2:
            one.append((flat(q, z, y, x), flat(q, 3 - z, y, x)))
        else:
            one.append((flat(q, z, y, x), flat(1 - q, z, y, x)))
            two.append((flat(q, z, y, x), flat(1 - q, 3 - z, y, x)))
    got_two = permute(low, two)
    got_one = permute(first, one)
    rows, width = top.shape
    vmem = pl.BlockSpec(memory_space=pltpu.VMEM)
    return pl.pallas_call(
        join_kernel,
        in_specs=[vmem] * 3,
        out_specs=vmem,
        out_shape=jax.ShapeDtypeStruct((rows, 2 * width - LANES), top.dtype),
        compiler_params=pltpu.CompilerParams(vmem_limit_bytes=2 << 20),
    )(top, got_one, got_two)


def gather_pieces(block):
    rows, _ = block.shape
    blocks = [block]
    for j in range(1, 8):
        pairs = []
        for q, z, y, x in everyone():
            m = near_mask(q)
            pairs.append((flat(q, z, y, x), flat(q, z ^ (m * (j & 1)), y ^ (m * ((j >> 1) & 1)), x ^ (m * (j >> 2)))))
        blocks.append(permute(block, pairs))
    whole = jnp.stack(blocks)
    third = rows // 3

    def swap(value, axis):
        pairs = []
        for q, z, y, x in everyone():
            n = [far_mask(q) if axis == i else 0 for i in range(3)]
            pairs.append((flat(q, z, y, x), flat(q, z ^ n[0], y ^ n[1], x ^ n[2])))
        return permute(value, pairs)

    pieces = [[whole[:, third * c : third * (c + 1)]] for c in range(3)]
    for step in range(3):
        count = len(pieces[0])
        for i in range(count):
            for c in range(3):
                pieces[c].append(swap(pieces[c][i], (c + step) % 3))
    return pieces


def per_device(master, gradient, first_moment, second_moment, max_norm, step_count):
    rows, cols = master.shape
    devices = 2 * RING**3
    f32 = jnp.float32
    state = jax.ShapeDtypeStruct((rows, cols), f32)
    vmem = pl.BlockSpec(memory_space=pltpu.VMEM)
    smem = pl.BlockSpec(memory_space=pltpu.SMEM)
    anywhere = pl.BlockSpec(memory_space=pl.ANY)
    own, known = pl.pallas_call(
        squares_kernel,
        in_specs=[smem, smem, vmem],
        out_specs=[vmem] * 2,
        out_shape=[jax.ShapeDtypeStruct((devices, LANES), f32), jax.ShapeDtypeStruct((8, LANES), f32)],
        compiler_params=pltpu.CompilerParams(vmem_limit_bytes=2 << 20),
    )(max_norm, step_count, gradient)
    sums = lax.all_to_all(own, AXES, 0, 0, tiled=True)

    half = jax.ShapeDtypeStruct((rows // 2, cols + LANES), jnp.bfloat16)
    new_master, new_first, new_second, top, low, first = pl.pallas_call(
        adam_kernel,
        in_specs=[vmem] * 6,
        out_specs=[vmem] * 6,
        out_shape=[state] * 3 + [half] * 3,
        compiler_params=pltpu.CompilerParams(vmem_limit_bytes=54600 << 10),
    )(sums, known, master, gradient, first_moment, second_moment)

    pieces = gather_pieces(redistribute(top, low, first))
    groups = rows * RING**3 // 2 // 8
    outs = ()
    for bits in ((0, 1, 2, 3), (4, 5, 6), (7,)):
        which = [(c, b) for b in bits for c in range(3)]
        outs = pl.pallas_call(
            functools.partial(place_kernel, which),
            in_specs=[anywhere] * (len(which) + len(outs)),
            out_specs=[anywhere] * 2,
            out_shape=[
                jax.ShapeDtypeStruct((groups, 8, 2 * cols), jnp.bfloat16),
                jax.ShapeDtypeStruct((groups, 8, LANES), jnp.bfloat16),
            ],
            input_output_aliases={len(which) + i: i for i in range(len(outs))},
            scratch_shapes=[pltpu.SemaphoreType.DMA],
            compiler_params=pltpu.CompilerParams(vmem_limit_bytes=1 << 20),
        )(*[pieces[c][b] for c, b in which], *outs)
    codes, scales = outs
    return (
        new_master,
        new_first,
        new_second,
        codes.reshape(groups * 8, 2 * cols),
        scales.reshape(groups * 8, LANES),
    )


def solution(mesh):
    finer = Mesh(mesh.devices.reshape(2, RING, RING, RING), AXES)
    state = P(SHARD, "pair")
    return jax.shard_map(
        per_device,
        mesh=finer,
        in_specs=(state, state, state, state, P(), P()),
        out_specs=(state, state, state, P("pair", None), P("pair", None)),
        check_vma=False,
    )
```

profile of v0, /device:TPU:0, one launch (start us, length us, event | category | flops | bytes accessed | tf_op | source)
XLA Modules:
  0.0 122.6 jit_solution(16715435931988426735)
XLA Ops:
  1.9 1.0 copy-done
  3.0 20.2 %all_to_all.11 = f32[128,1,128]{2,1,0:T(1,128)S(1)} all-to-all(f32[128,1,128]{2,1,0:T(1,128)S(1)} %bitcast.23), channel_id=1, replica_groups=mesh['pair'=2,'shard_0'=4,'shard_1'=4,'shard_2'=4] {'pair','shard_0','sh..., dimensions={0} | all-to-all | bytes 131072 | tf_op jit(solution)/shard_map/all_to_all | solution.py:229
  23.1 2.9 %shard_map.102 = (f32[48,2048]{1,0:T(8,128)}, f32[48,2048]{1,0:T(8,128)}, f32[48,2048]{1,0:T(8,128)}, bf16[24,2176]{1,0:T(8,128)(2,1)S(1)}, bf16[24,2176]{1,0:T(8,128)(2,1)S(1)}, /*index=5*/bf16[24,2176]{1,0:T(8,128)(2,1)S(1)}) custom-call(f32[128,128]{1,0:T(8,128)S(1)} %bitcast.22, f32[8,128]{1,0:T(8,128)S(1)} %get-tuple-element.20.known_ref, ...), custom_call_target="tpu_custom_call" | custom-call | tf_op jit(solution)/shard_map/pallas_call | solution.py:232
  26.1 0.9 collective-permute-start
  26.9 0.7 collective-permute-start.1
  27.6 1.6 %collective-permute-done.one_ref = bf16[24,2176]{1,0:T(8,128)(2,1)S(1)} collective-permute-done((bf16[24,2176]{1,0:T(8,128)(2,1)S(1)}, bf16[24,2176]{1,0:T(8,128)(2,1)S(1)}, u32[]{:S(2)}, u32[]{:S(2)}) %collective-permute-start) | collective-permute-done | bytes 104480 | tf_op jit(solution)/shard_map/ppermute | solution.py:162
  29.3 0.8 collective-permute-start.8
  30.0 2.3 %collective-permute-start.7 = (bf16[24,4224]{1,0:T(8,128)(2,1)S(1)}, bf16[24,4224]{1,0:T(8,128)(2,1)S(1)}, u32[]{:S(2)}, u32[]{:S(2)}) collective-permute-start(bf16[24,4224]{1,0:T(8,128)(2,1)S(1)} %shard_map.103), channel_id=1, source_target_pairs={{0,5},{1,4},{2,7},{3,6},{4,1},{5,0},{6,3},{7,2},{8,13},{9,12},{10,... | collective-permute-start | bytes 608264 | tf_op jit(solution)/shard_map/ppermute | solution.py:162
  32.3 1.4 %collective-permute-start.6 = (bf16[24,4224]{1,0:T(8,128)(2,1)S(1)}, bf16[24,4224]{1,0:T(8,128)(2,1)S(1)}, u32[]{:S(2)}, u32[]{:S(2)}) collective-permute-start(bf16[24,4224]{1,0:T(8,128)(2,1)S(1)} %shard_map.103), channel_id=1, source_target_pairs={{0,17},{1,16},{2,19},{3,18},{4,21},{5,20},{6,23},{7,22},{8,25},{9,... | collective-permute-start | bytes 608264 | tf_op jit(solution)/shard_map/ppermute | solution.py:162
  33.7 1.4 %collective-permute-start.5 = (bf16[24,4224]{1,0:T(8,128)(2,1)S(1)}, bf16[24,4224]{1,0:T(8,128)(2,1)S(1)}, u32[]{:S(2)}, u32[]{:S(2)}) collective-permute-start(bf16[24,4224]{1,0:T(8,128)(2,1)S(1)} %shard_map.103), channel_id=1, source_target_pairs={{0,1},{1,0},{2,3},{3,2},{4,5},{5,4},{6,7},{7,6},{8,9},{9,8},{10,11... | collective-permute-start | bytes 608264 | tf_op jit(solution)/shard_map/ppermute | solution.py:162
  35.2 0.6 collective-permute-start.2
  35.8 6.8 %collective-permute-done.2 = bf16[24,4224]{1,0:T(8,128)(2,1)S(1)} collective-permute-done((bf16[24,4224]{1,0:T(8,128)(2,1)S(1)}, bf16[24,4224]{1,0:T(8,128)(2,1)S(1)}, u32[]{:S(2)}, u32[]{:S(2)}) %collective-permute-start.2) | collective-permute-done | bytes 202784 | tf_op jit(solution)/shard_map/ppermute | solution.py:162
  42.6 1.2 collective-permute-start.3
  43.7 4.5 %collective-permute-done.3 = bf16[24,4224]{1,0:T(8,128)(2,1)S(1)} collective-permute-done((bf16[24,4224]{1,0:T(8,128)(2,1)S(1)}, bf16[24,4224]{1,0:T(8,128)(2,1)S(1)}, u32[]{:S(2)}, u32[]{:S(2)}) %collective-permute-start.3) | collective-permute-done | bytes 202784 | tf_op jit(solution)/shard_map/ppermute | solution.py:162
  48.3 1.2 collective-permute-start.4
  49.5 5.4 %collective-permute-done.4 = bf16[24,4224]{1,0:T(8,128)(2,1)S(1)} collective-permute-done((bf16[24,4224]{1,0:T(8,128)(2,1)S(1)}, bf16[24,4224]{1,0:T(8,128)(2,1)S(1)}, u32[]{:S(2)}, u32[]{:S(2)}) %collective-permute-start.4) | collective-permute-done | bytes 202784 | tf_op jit(solution)/shard_map/ppermute | solution.py:162
  55.2 5.0 %collective-permute-start.28 = (bf16[8,8,4224]{2,1,0:T(8,128)(2,1)S(1)}, bf16[8,8,4224]{2,1,0:T(8,128)(2,1)S(1)}, u32[]{:S(2)}, u32[]{:S(2)}) collective-permute-start(bf16[8,8,4224]{2,1,0:T(8,128)(2,1)S(1)} %get-tuple-element.33.refs_2_), channel_id=1, source_target_pairs={{0,48},{1,49},{2,50},{3,51},{4,52},{5,53},{6,54},{7,55},{8,56},{9,... | collective-permute-start | bytes 1622024 | tf_op jit(solution)/shard_map/ppermute | solution.py:162
  60.2 1.3 %collective-permute-start.20 = (bf16[8,8,4224]{2,1,0:T(8,128)(2,1)S(1)}, bf16[8,8,4224]{2,1,0:T(8,128)(2,1)S(1)}, u32[]{:S(2)}, u32[]{:S(2)}) collective-permute-start(bf16[8,8,4224]{2,1,0:T(8,128)(2,1)S(1)} %get-tuple-element.33.refs_2_), channel_id=1, source_target_pairs={{0,12},{1,13},{2,14},{3,15},{4,8},{5,9},{6,10},{7,11},{8,4},{9,5},... | collective-permute-start | bytes 1622024 | tf_op jit(solution)/shard_map/ppermute | solution.py:162
  61.5 0.9 collective-permute-start.15
  62.4 2.4 %collective-permute-start.26 = (bf16[8,8,4224]{2,1,0:T(8,128)(2,1)S(1)}, bf16[8,8,4224]{2,1,0:T(8,128)(2,1)S(1)}, u32[]{:S(2)}, u32[]{:S(2)}) collective-permute-start(bf16[8,8,4224]{2,1,0:T(8,128)(2,1)S(1)} %get-tuple-element.34.refs_1_), channel_id=1, source_target_pairs={{0,3},{1,2},{2,1},{3,0},{4,7},{5,6},{6,5},{7,4},{8,11},{9,10},{10,... | collective-permute-start | bytes 1622024 | tf_op jit(solution)/shard_map/ppermute | solution.py:162
  64.8 4.1 %collective-permute-done.28.refs_8_ = bf16[8,8,4224]{2,1,0:T(8,128)(2,1)S(1)} collective-permute-done((bf16[8,8,4224]{2,1,0:T(8,128)(2,1)S(1)}, bf16[8,8,4224]{2,1,0:T(8,128)(2,1)S(1)}, u32[]{:S(2)}, u32[]{:S(2)}) %collective-permute-start.28) | collective-permute-done | bytes 540704 | tf_op jit(solution)/shard_map/ppermute | solution.py:162
  68.9 1.7 %collective-permute-start.12 = (bf16[8,8,4224]{2,1,0:T(8,128)(2,1)S(1)}, bf16[8,8,4224]{2,1,0:T(8,128)(2,1)S(1)}, u32[]{:S(2)}, u32[]{:S(2)}) collective-permute-start(bf16[8,8,4224]{2,1,0:T(8,128)(2,1)S(1)} %get-tuple-element.34.refs_1_), channel_id=1, source_target_pairs={{0,12},{1,13},{2,14},{3,15},{4,8},{5,9},{6,10},{7,11},{8,4},{9,5},... | collective-permute-start | bytes 1622024 | tf_op jit(solution)/shard_map/ppermute | solution.py:162
  70.8 1.4 %collective-permute-start.24 = (bf16[8,8,4224]{2,1,0:T(8,128)(2,1)S(1)}, bf16[8,8,4224]{2,1,0:T(8,128)(2,1)S(1)}, u32[]{:S(2)}, u32[]{:S(2)}) collective-permute-start(bf16[8,8,4224]{2,1,0:T(8,128)(2,1)S(1)} %get-tuple-element.35.refs_0_), channel_id=1, source_target_pairs={{0,12},{1,13},{2,14},{3,15},{4,8},{5,9},{6,10},{7,11},{8,4},{9,5},... | collective-permute-start | bytes 1622024 | tf_op jit(solution)/shard_map/ppermute | solution.py:162
  72.2 1.9 %collective-permute-start.18 = (bf16[8,8,4224]{2,1,0:T(8,128)(2,1)S(1)}, bf16[8,8,4224]{2,1,0:T(8,128)(2,1)S(1)}, u32[]{:S(2)}, u32[]{:S(2)}) collective-permute-start(bf16[8,8,4224]{2,1,0:T(8,128)(2,1)S(1)} %get-tuple-element.35.refs_0_), channel_id=1, source_target_pairs={{0,3},{1,2},{2,1},{3,0},{4,7},{5,6},{6,5},{7,4},{8,11},{9,10},{10,... | collective-permute-start | bytes 1622024 | tf_op jit(solution)/shard_map/ppermute | solution.py:162
  74.1 3.8 %collective-permute-done.26.refs_7_ = bf16[8,8,4224]{2,1,0:T(8,128)(2,1)S(1)} collective-permute-done((bf16[8,8,4224]{2,1,0:T(8,128)(2,1)S(1)}, bf16[8,8,4224]{2,1,0:T(8,128)(2,1)S(1)}, u32[]{:S(2)}, u32[]{:S(2)}) %collective-permute-start.26) | collective-permute-done | bytes 540704 | tf_op jit(solution)/shard_map/ppermute | solution.py:162
  78.0 2.0 %collective-permute-start.29 = (bf16[8,8,4224]{2,1,0:T(8,128)(2,1)S(1)}, bf16[8,8,4224]{2,1,0:T(8,128)(2,1)S(1)}, u32[]{:S(2)}, u32[]{:S(2)}) collective-permute-start(bf16[8,8,4224]{2,1,0:T(8,128)(2,1)S(1)} %collective-permute-done.28.refs_8_), channel_id=1, source_target_pairs={{0,12},{1,13},{2,14},{3,15},{4,8},{5,9},{6,10},{7,11},{8,4},{9,5},... | collective-permute-start | bytes 1622024 | tf_op jit(solution)/shard_map/ppermute | solution.py:162
  79.9 1.3 %collective-permute-start.23 = (bf16[8,8,4224]{2,1,0:T(8,128)(2,1)S(1)}, bf16[8,8,4224]{2,1,0:T(8,128)(2,1)S(1)}, u32[]{:S(2)}, u32[]{:S(2)}) collective-permute-start(bf16[8,8,4224]{2,1,0:T(8,128)(2,1)S(1)} %collective-permute-done.15.refs_5_), channel_id=1, source_target_pairs={{0,12},{1,13},{2,14},{3,15},{4,8},{5,9},{6,10},{7,11},{8,4},{9,5},... | collective-permute-start | bytes 1622024 | tf_op jit(solution)/shard_map/ppermute | solution.py:162
  81.2 4.1 %collective-permute-done.24.refs_6_ = bf16[8,8,4224]{2,1,0:T(8,128)(2,1)S(1)} collective-permute-done((bf16[8,8,4224]{2,1,0:T(8,128)(2,1)S(1)}, bf16[8,8,4224]{2,1,0:T(8,128)(2,1)S(1)}, u32[]{:S(2)}, u32[]{:S(2)}) %collective-permute-start.24) | collective-permute-done | bytes 540704 | tf_op jit(solution)/shard_map/ppermute | solution.py:162
  85.3 2.2 %collective-permute-start.16 = (bf16[8,8,4224]{2,1,0:T(8,128)(2,1)S(1)}, bf16[8,8,4224]{2,1,0:T(8,128)(2,1)S(1)}, u32[]{:S(2)}, u32[]{:S(2)}) collective-permute-start(bf16[8,8,4224]{2,1,0:T(8,128)(2,1)S(1)} %collective-permute-done.15.refs_5_), channel_id=1, source_target_pairs={{0,48},{1,49},{2,50},{3,51},{4,52},{5,53},{6,54},{7,55},{8,56},{9,... | collective-permute-start | bytes 1622024 | tf_op jit(solution)/shard_map/ppermute | solution.py:162
  87.4 1.1 collective-permute-start.27
  88.5 2.2 %collective-permute-start.22 = (bf16[8,8,4224]{2,1,0:T(8,128)(2,1)S(1)}, bf16[8,8,4224]{2,1,0:T(8,128)(2,1)S(1)}, u32[]{:S(2)}, u32[]{:S(2)}) collective-permute-start(bf16[8,8,4224]{2,1,0:T(8,128)(2,1)S(1)} %collective-permute-done.12.refs_4_), channel_id=1, source_target_pairs={{0,48},{1,49},{2,50},{3,51},{4,52},{5,53},{6,54},{7,55},{8,56},{9,... | collective-permute-start | bytes 1622024 | tf_op jit(solution)/shard_map/ppermute | solution.py:162
  90.7 0.4 collective-permute-done.29.refs_8_
  91.1 1.9 %collective-permute-start.13 = (bf16[8,8,4224]{2,1,0:T(8,128)(2,1)S(1)}, bf16[8,8,4224]{2,1,0:T(8,128)(2,1)S(1)}, u32[]{:S(2)}, u32[]{:S(2)}) collective-permute-start(bf16[8,8,4224]{2,1,0:T(8,128)(2,1)S(1)} %collective-permute-done.12.refs_4_), channel_id=1, source_target_pairs={{0,3},{1,2},{2,1},{3,0},{4,7},{5,6},{6,5},{7,4},{8,11},{9,10},{10,... | collective-permute-start | bytes 1622024 | tf_op jit(solution)/shard_map/ppermute | solution.py:162
  93.0 3.8 %collective-permute-done.23.refs_5_ = bf16[8,8,4224]{2,1,0:T(8,128)(2,1)S(1)} collective-permute-done((bf16[8,8,4224]{2,1,0:T(8,128)(2,1)S(1)}, bf16[8,8,4224]{2,1,0:T(8,128)(2,1)S(1)}, u32[]{:S(2)}, u32[]{:S(2)}) %collective-permute-start.23) | collective-permute-done | bytes 540704 | tf_op jit(solution)/shard_map/ppermute | solution.py:162
  96.9 1.7 %collective-permute-start.10 = (bf16[8,8,4224]{2,1,0:T(8,128)(2,1)S(1)}, bf16[8,8,4224]{2,1,0:T(8,128)(2,1)S(1)}, u32[]{:S(2)}, u32[]{:S(2)}) collective-permute-start(bf16[8,8,4224]{2,1,0:T(8,128)(2,1)S(1)} %collective-permute-done.9.refs_3_), channel_id=1, source_target_pairs={{0,12},{1,13},{2,14},{3,15},{4,8},{5,9},{6,10},{7,11},{8,4},{9,5},... | collective-permute-start | bytes 1622024 | tf_op jit(solution)/shard_map/ppermute | solution.py:162
  98.6 1.2 %collective-permute-start.25 = (bf16[8,8,4224]{2,1,0:T(8,128)(2,1)S(1)}, bf16[8,8,4224]{2,1,0:T(8,128)(2,1)S(1)}, u32[]{:S(2)}, u32[]{:S(2)}) collective-permute-start(bf16[8,8,4224]{2,1,0:T(8,128)(2,1)S(1)} %collective-permute-done.24.refs_6_), channel_id=1, source_target_pairs={{0,3},{1,2},{2,1},{3,0},{4,7},{5,6},{6,5},{7,4},{8,11},{9,10},{10,... | collective-permute-start | bytes 1622024 | tf_op jit(solution)/shard_map/ppermute | solution.py:162
  99.8 1.8 %collective-permute-done.27.refs_7_ = bf16[8,8,4224]{2,1,0:T(8,128)(2,1)S(1)} collective-permute-done((bf16[8,8,4224]{2,1,0:T(8,128)(2,1)S(1)}, bf16[8,8,4224]{2,1,0:T(8,128)(2,1)S(1)}, u32[]{:S(2)}, u32[]{:S(2)}) %collective-permute-start.27) | collective-permute-done | bytes 540704 | tf_op jit(solution)/shard_map/ppermute | solution.py:162
  101.6 1.9 %collective-permute-start.21 = (bf16[8,8,4224]{2,1,0:T(8,128)(2,1)S(1)}, bf16[8,8,4224]{2,1,0:T(8,128)(2,1)S(1)}, u32[]{:S(2)}, u32[]{:S(2)}) collective-permute-start(bf16[8,8,4224]{2,1,0:T(8,128)(2,1)S(1)} %collective-permute-done.9.refs_3_), channel_id=1, source_target_pairs={{0,3},{1,2},{2,1},{3,0},{4,7},{5,6},{6,5},{7,4},{8,11},{9,10},{10,... | collective-permute-start | bytes 1622024 | tf_op jit(solution)/shard_map/ppermute | solution.py:162
  103.6 3.8 %collective-permute-done.22.refs_4_ = bf16[8,8,4224]{2,1,0:T(8,128)(2,1)S(1)} collective-permute-done((bf16[8,8,4224]{2,1,0:T(8,128)(2,1)S(1)}, bf16[8,8,4224]{2,1,0:T(8,128)(2,1)S(1)}, u32[]{:S(2)}, u32[]{:S(2)}) %collective-permute-start.22) | collective-permute-done | bytes 540704 | tf_op jit(solution)/shard_map/ppermute | solution.py:162
  107.4 1.7 %collective-permute-start.17 = (bf16[8,8,4224]{2,1,0:T(8,128)(2,1)S(1)}, bf16[8,8,4224]{2,1,0:T(8,128)(2,1)S(1)}, u32[]{:S(2)}, u32[]{:S(2)}) collective-permute-start(bf16[8,8,4224]{2,1,0:T(8,128)(2,1)S(1)} %collective-permute-done.16.refs_11_), channel_id=1, source_target_pairs={{0,12},{1,13},{2,14},{3,15},{4,8},{5,9},{6,10},{7,11},{8,4},{9,5},... | collective-permute-start | bytes 1622024 | tf_op jit(solution)/shard_map/ppermute | solution.py:162
  109.2 1.6 %collective-permute-start.14 = (bf16[8,8,4224]{2,1,0:T(8,128)(2,1)S(1)}, bf16[8,8,4224]{2,1,0:T(8,128)(2,1)S(1)}, u32[]{:S(2)}, u32[]{:S(2)}) collective-permute-start(bf16[8,8,4224]{2,1,0:T(8,128)(2,1)S(1)} %collective-permute-done.13.refs_10_), channel_id=1, source_target_pairs={{0,48},{1,49},{2,50},{3,51},{4,52},{5,53},{6,54},{7,55},{8,56},{9,... | collective-permute-start | bytes 1622024 | tf_op jit(solution)/shard_map/ppermute | solution.py:162
  110.8 1.2 collective-permute-start.11
  112.0 2.9 %shard_map.104 = (bf16[192,8,4096]{2,1,0:T(8,128)(2,1)}, bf16[192,8,128]{2,1,0:T(8,128)(2,1)}) custom-call(bf16[8,8,4224]{2,1,0:T(8,128)(2,1)S(1)} %get-tuple-element.35.refs_0_, bf16[8,8,4224]{2,1,0:T(8,128)(2,1)S(1)} %get-tuple-element.34.refs_1_, bf16[8,8,4224]{2,1,0:T(8,128)(2,1)S(1)} %get-tuple-element.33.refs_2_, ...), custom_call_target="tpu_custom_call" | custom-call | tf_op jit(solution)/shard_map/pallas_call | solution.py:245
  115.0 2.4 %shard_map.105 = (bf16[192,8,4096]{2,1,0:T(8,128)(2,1)}, bf16[192,8,128]{2,1,0:T(8,128)(2,1)}) custom-call(bf16[8,8,4224]{2,1,0:T(8,128)(2,1)S(1)} %collective-permute-done.18.refs_0_, bf16[8,8,4224]{2,1,0:T(8,128)(2,1)S(1)} %collective-permute-done.19.refs_1_, ...), custom_call_target="tpu_custom_call", output_to_operand_aliasing={{0}: (9, {}), {1}: (10, {})} | custom-call | tf_op jit(solution)/shard_map/pallas_call | solution.py:245
  117.4 0.6 collective-permute-done.17.refs_2_
  118.0 1.7 %collective-permute-done.14.refs_1_ = bf16[8,8,4224]{2,1,0:T(8,128)(2,1)S(1)} collective-permute-done((bf16[8,8,4224]{2,1,0:T(8,128)(2,1)S(1)}, bf16[8,8,4224]{2,1,0:T(8,128)(2,1)S(1)}, u32[]{:S(2)}, u32[]{:S(2)}) %collective-permute-start.14) | collective-permute-done | bytes 540704 | tf_op jit(solution)/shard_map/ppermute | solution.py:162
  119.7 1.6 %collective-permute-done.11.refs_0_ = bf16[8,8,4224]{2,1,0:T(8,128)(2,1)S(1)} collective-permute-done((bf16[8,8,4224]{2,1,0:T(8,128)(2,1)S(1)}, bf16[8,8,4224]{2,1,0:T(8,128)(2,1)S(1)}, u32[]{:S(2)}, u32[]{:S(2)}) %collective-permute-start.11) | collective-permute-done | bytes 540704 | tf_op jit(solution)/shard_map/ppermute | solution.py:162
  121.4 1.2 shard_map.106
  (30 shorter events, 0.8 us)
Async XLA Ops:
  1.9 1.0 copy-start
  26.1 3.2 %collective-permute-start = (bf16[24,2176]{1,0:T(8,128)(2,1)S(1)}, bf16[24,2176]{1,0:T(8,128)(2,1)S(1)}, u32[]{:S(2)}, u32[]{:S(2)}) collective-permute-start(bf16[24,2176]{1,0:T(8,128)(2,1)S(1)} %get-tuple-element.25), channel_id=1, source_target_pairs={{0,48},{1,49},{2,50},{3,51},{4,52},{5,53},{6,54},{7,55},{8,56},{9,... | collective-permute-start | bytes 313352 | tf_op jit(solution)/shard_map/ppermute | solution.py:162
  26.9 2.3 %collective-permute-start.1 = (bf16[24,2176]{1,0:T(8,128)(2,1)S(1)}, bf16[24,2176]{1,0:T(8,128)(2,1)S(1)}, u32[]{:S(2)}, u32[]{:S(2)}) collective-permute-start(bf16[24,2176]{1,0:T(8,128)(2,1)S(1)} %get-tuple-element.26), channel_id=1, source_target_pairs={{32,80},{33,81},{34,82},{35,83},{36,84},{37,85},{38,86},{39,87},{4... | collective-permute-start | bytes 313352 | tf_op jit(solution)/shard_map/ppermute | solution.py:162
  29.3 25.8 %collective-permute-start.8 = (bf16[24,4224]{1,0:T(8,128)(2,1)S(1)}, bf16[24,4224]{1,0:T(8,128)(2,1)S(1)}, u32[]{:S(2)}, u32[]{:S(2)}) collective-permute-start(bf16[24,4224]{1,0:T(8,128)(2,1)S(1)} %shard_map.103), channel_id=1, source_target_pairs={{0,21},{1,20},{2,23},{3,22},{4,17},{5,16},{6,19},{7,18},{8,29},{9,... | collective-permute-start | bytes 608264 | tf_op jit(solution)/shard_map/ppermute | solution.py:162
  30.0 25.0 %collective-permute-start.7 = (bf16[24,4224]{1,0:T(8,128)(2,1)S(1)}, bf16[24,4224]{1,0:T(8,128)(2,1)S(1)}, u32[]{:S(2)}, u32[]{:S(2)}) collective-permute-start(bf16[24,4224]{1,0:T(8,128)(2,1)S(1)} %shard_map.103), channel_id=1, source_target_pairs={{0,5},{1,4},{2,7},{3,6},{4,1},{5,0},{6,3},{7,2},{8,13},{9,12},{10,... | collective-permute-start | bytes 608264 | tf_op jit(solution)/shard_map/ppermute | solution.py:162
  32.3 22.7 %collective-permute-start.6 = (bf16[24,4224]{1,0:T(8,128)(2,1)S(1)}, bf16[24,4224]{1,0:T(8,128)(2,1)S(1)}, u32[]{:S(2)}, u32[]{:S(2)}) collective-permute-start(bf16[24,4224]{1,0:T(8,128)(2,1)S(1)} %shard_map.103), channel_id=1, source_target_pairs={{0,17},{1,16},{2,19},{3,18},{4,21},{5,20},{6,23},{7,22},{8,25},{9,... | collective-permute-start | bytes 608264 | tf_op jit(solution)/shard_map/ppermute | solution.py:162
  33.7 21.2 %collective-permute-start.5 = (bf16[24,4224]{1,0:T(8,128)(2,1)S(1)}, bf16[24,4224]{1,0:T(8,128)(2,1)S(1)}, u32[]{:S(2)}, u32[]{:S(2)}) collective-permute-start(bf16[24,4224]{1,0:T(8,128)(2,1)S(1)} %shard_map.103), channel_id=1, source_target_pairs={{0,1},{1,0},{2,3},{3,2},{4,5},{5,4},{6,7},{7,6},{8,9},{9,8},{10,11... | collective-permute-start | bytes 608264 | tf_op jit(solution)/shard_map/ppermute | solution.py:162
  35.2 7.4 %collective-permute-start.2 = (bf16[24,4224]{1,0:T(8,128)(2,1)S(1)}, bf16[24,4224]{1,0:T(8,128)(2,1)S(1)}, u32[]{:S(2)}, u32[]{:S(2)}) collective-permute-start(bf16[24,4224]{1,0:T(8,128)(2,1)S(1)} %shard_map.103), channel_id=1, source_target_pairs={{0,16},{1,17},{2,18},{3,19},{4,20},{5,21},{6,22},{7,23},{8,24},{9,... | collective-permute-start | bytes 608264 | tf_op jit(solution)/shard_map/ppermute | solution.py:162
  42.6 5.7 %collective-permute-start.3 = (bf16[24,4224]{1,0:T(8,128)(2,1)S(1)}, bf16[24,4224]{1,0:T(8,128)(2,1)S(1)}, u32[]{:S(2)}, u32[]{:S(2)}) collective-permute-start(bf16[24,4224]{1,0:T(8,128)(2,1)S(1)} %shard_map.103), channel_id=1, source_target_pairs={{0,4},{1,5},{2,6},{3,7},{4,0},{5,1},{6,2},{7,3},{8,12},{9,13},{10,... | collective-permute-start | bytes 608264 | tf_op jit(solution)/shard_map/ppermute | solution.py:162
  48.3 6.6 %collective-permute-start.4 = (bf16[24,4224]{1,0:T(8,128)(2,1)S(1)}, bf16[24,4224]{1,0:T(8,128)(2,1)S(1)}, u32[]{:S(2)}, u32[]{:S(2)}) collective-permute-start(bf16[24,4224]{1,0:T(8,128)(2,1)S(1)} %shard_map.103), channel_id=1, source_target_pairs={{0,20},{1,21},{2,22},{3,23},{4,16},{5,17},{6,18},{7,19},{8,28},{9,... | collective-permute-start | bytes 608264 | tf_op jit(solution)/shard_map/ppermute | solution.py:162
  55.2 13.7 %collective-permute-start.28 = (bf16[8,8,4224]{2,1,0:T(8,128)(2,1)S(1)}, bf16[8,8,4224]{2,1,0:T(8,128)(2,1)S(1)}, u32[]{:S(2)}, u32[]{:S(2)}) collective-permute-start(bf16[8,8,4224]{2,1,0:T(8,128)(2,1)S(1)} %get-tuple-element.33.refs_2_), channel_id=1, source_target_pairs={{0,48},{1,49},{2,50},{3,51},{4,52},{5,53},{6,54},{7,55},{8,56},{9,... | collective-permute-start | bytes 1622024 | tf_op jit(solution)/shard_map/ppermute | solution.py:162
  60.2 10.6 %collective-permute-start.20 = (bf16[8,8,4224]{2,1,0:T(8,128)(2,1)S(1)}, bf16[8,8,4224]{2,1,0:T(8,128)(2,1)S(1)}, u32[]{:S(2)}, u32[]{:S(2)}) collective-permute-start(bf16[8,8,4224]{2,1,0:T(8,128)(2,1)S(1)} %get-tuple-element.33.refs_2_), channel_id=1, source_target_pairs={{0,12},{1,13},{2,14},{3,15},{4,8},{5,9},{6,10},{7,11},{8,4},{9,5},... | collective-permute-start | bytes 1622024 | tf_op jit(solution)/shard_map/ppermute | solution.py:162
  61.5 10.7 %collective-permute-start.15 = (bf16[8,8,4224]{2,1,0:T(8,128)(2,1)S(1)}, bf16[8,8,4224]{2,1,0:T(8,128)(2,1)S(1)}, u32[]{:S(2)}, u32[]{:S(2)}) collective-permute-start(bf16[8,8,4224]{2,1,0:T(8,128)(2,1)S(1)} %get-tuple-element.33.refs_2_), channel_id=1, source_target_pairs={{0,3},{1,2},{2,1},{3,0},{4,7},{5,6},{6,5},{7,4},{8,11},{9,10},{10,... | collective-permute-start | bytes 1622024 | tf_op jit(solution)/shard_map/ppermute | solution.py:162
  62.4 15.5 %collective-permute-start.26 = (bf16[8,8,4224]{2,1,0:T(8,128)(2,1)S(1)}, bf16[8,8,4224]{2,1,0:T(8,128)(2,1)S(1)}, u32[]{:S(2)}, u32[]{:S(2)}) collective-permute-start(bf16[8,8,4224]{2,1,0:T(8,128)(2,1)S(1)} %get-tuple-element.34.refs_1_), channel_id=1, source_target_pairs={{0,3},{1,2},{2,1},{3,0},{4,7},{5,6},{6,5},{7,4},{8,11},{9,10},{10,... | collective-permute-start | bytes 1622024 | tf_op jit(solution)/shard_map/ppermute | solution.py:162
  64.7 13.2 %collective-permute-start.19 = (bf16[8,8,4224]{2,1,0:T(8,128)(2,1)S(1)}, bf16[8,8,4224]{2,1,0:T(8,128)(2,1)S(1)}, u32[]{:S(2)}, u32[]{:S(2)}) collective-permute-start(bf16[8,8,4224]{2,1,0:T(8,128)(2,1)S(1)} %get-tuple-element.34.refs_1_), channel_id=1, source_target_pairs={{0,48},{1,49},{2,50},{3,51},{4,52},{5,53},{6,54},{7,55},{8,56},{9,... | collective-permute-start | bytes 1622024 | tf_op jit(solution)/shard_map/ppermute | solution.py:162
  68.9 11.0 %collective-permute-start.12 = (bf16[8,8,4224]{2,1,0:T(8,128)(2,1)S(1)}, bf16[8,8,4224]{2,1,0:T(8,128)(2,1)S(1)}, u32[]{:S(2)}, u32[]{:S(2)}) collective-permute-start(bf16[8,8,4224]{2,1,0:T(8,128)(2,1)S(1)} %get-tuple-element.34.refs_1_), channel_id=1, source_target_pairs={{0,12},{1,13},{2,14},{3,15},{4,8},{5,9},{6,10},{7,11},{8,4},{9,5},... | collective-permute-start | bytes 1622024 | tf_op jit(solution)/shard_map/ppermute | solution.py:162
  70.8 14.5 %collective-permute-start.24 = (bf16[8,8,4224]{2,1,0:T(8,128)(2,1)S(1)}, bf16[8,8,4224]{2,1,0:T(8,128)(2,1)S(1)}, u32[]{:S(2)}, u32[]{:S(2)}) collective-permute-start(bf16[8,8,4224]{2,1,0:T(8,128)(2,1)S(1)} %get-tuple-element.35.refs_0_), channel_id=1, source_target_pairs={{0,12},{1,13},{2,14},{3,15},{4,8},{5,9},{6,10},{7,11},{8,4},{9,5},... | collective-permute-start | bytes 1622024 | tf_op jit(solution)/shard_map/ppermute | solution.py:162
  72.2 15.3 %collective-permute-start.18 = (bf16[8,8,4224]{2,1,0:T(8,128)(2,1)S(1)}, bf16[8,8,4224]{2,1,0:T(8,128)(2,1)S(1)}, u32[]{:S(2)}, u32[]{:S(2)}) collective-permute-start(bf16[8,8,4224]{2,1,0:T(8,128)(2,1)S(1)} %get-tuple-element.35.refs_0_), channel_id=1, source_target_pairs={{0,3},{1,2},{2,1},{3,0},{4,7},{5,6},{6,5},{7,4},{8,11},{9,10},{10,... | collective-permute-start | bytes 1622024 | tf_op jit(solution)/shard_map/ppermute | solution.py:162
  77.9 10.7 %collective-permute-start.9 = (bf16[8,8,4224]{2,1,0:T(8,128)(2,1)S(1)}, bf16[8,8,4224]{2,1,0:T(8,128)(2,1)S(1)}, u32[]{:S(2)}, u32[]{:S(2)}) collective-permute-start(bf16[8,8,4224]{2,1,0:T(8,128)(2,1)S(1)} %get-tuple-element.35.refs_0_), channel_id=1, source_target_pairs={{0,48},{1,49},{2,50},{3,51},{4,52},{5,53},{6,54},{7,55},{8,56},{9,... | collective-permute-start | bytes 1622024 | tf_op jit(solution)/shard_map/ppermute | solution.py:162
  78.0 13.1 %collective-permute-start.29 = (bf16[8,8,4224]{2,1,0:T(8,128)(2,1)S(1)}, bf16[8,8,4224]{2,1,0:T(8,128)(2,1)S(1)}, u32[]{:S(2)}, u32[]{:S(2)}) collective-permute-start(bf16[8,8,4224]{2,1,0:T(8,128)(2,1)S(1)} %collective-permute-done.28.refs_8_), channel_id=1, source_target_pairs={{0,12},{1,13},{2,14},{3,15},{4,8},{5,9},{6,10},{7,11},{8,4},{9,5},... | collective-permute-start | bytes 1622024 | tf_op jit(solution)/shard_map/ppermute | solution.py:162
  79.9 16.9 %collective-permute-start.23 = (bf16[8,8,4224]{2,1,0:T(8,128)(2,1)S(1)}, bf16[8,8,4224]{2,1,0:T(8,128)(2,1)S(1)}, u32[]{:S(2)}, u32[]{:S(2)}) collective-permute-start(bf16[8,8,4224]{2,1,0:T(8,128)(2,1)S(1)} %collective-permute-done.15.refs_5_), channel_id=1, source_target_pairs={{0,12},{1,13},{2,14},{3,15},{4,8},{5,9},{6,10},{7,11},{8,4},{9,5},... | collective-permute-start | bytes 1622024 | tf_op jit(solution)/shard_map/ppermute | solution.py:162
  85.3 13.3 %collective-permute-start.16 = (bf16[8,8,4224]{2,1,0:T(8,128)(2,1)S(1)}, bf16[8,8,4224]{2,1,0:T(8,128)(2,1)S(1)}, u32[]{:S(2)}, u32[]{:S(2)}) collective-permute-start(bf16[8,8,4224]{2,1,0:T(8,128)(2,1)S(1)} %collective-permute-done.15.refs_5_), channel_id=1, source_target_pairs={{0,48},{1,49},{2,50},{3,51},{4,52},{5,53},{6,54},{7,55},{8,56},{9,... | collective-permute-start | bytes 1622024 | tf_op jit(solution)/shard_map/ppermute | solution.py:162
  87.4 14.2 %collective-permute-start.27 = (bf16[8,8,4224]{2,1,0:T(8,128)(2,1)S(1)}, bf16[8,8,4224]{2,1,0:T(8,128)(2,1)S(1)}, u32[]{:S(2)}, u32[]{:S(2)}) collective-permute-start(bf16[8,8,4224]{2,1,0:T(8,128)(2,1)S(1)} %collective-permute-done.26.refs_7_), channel_id=1, source_target_pairs={{0,48},{1,49},{2,50},{3,51},{4,52},{5,53},{6,54},{7,55},{8,56},{9,... | collective-permute-start | bytes 1622024 | tf_op jit(solution)/shard_map/ppermute | solution.py:162
  88.5 18.9 %collective-permute-start.22 = (bf16[8,8,4224]{2,1,0:T(8,128)(2,1)S(1)}, bf16[8,8,4224]{2,1,0:T(8,128)(2,1)S(1)}, u32[]{:S(2)}, u32[]{:S(2)}) collective-permute-start(bf16[8,8,4224]{2,1,0:T(8,128)(2,1)S(1)} %collective-permute-done.12.refs_4_), channel_id=1, source_target_pairs={{0,48},{1,49},{2,50},{3,51},{4,52},{5,53},{6,54},{7,55},{8,56},{9,... | collective-permute-start | bytes 1622024 | tf_op jit(solution)/shard_map/ppermute | solution.py:162
  91.1 18.1 %collective-permute-start.13 = (bf16[8,8,4224]{2,1,0:T(8,128)(2,1)S(1)}, bf16[8,8,4224]{2,1,0:T(8,128)(2,1)S(1)}, u32[]{:S(2)}, u32[]{:S(2)}) collective-permute-start(bf16[8,8,4224]{2,1,0:T(8,128)(2,1)S(1)} %collective-permute-done.12.refs_4_), channel_id=1, source_target_pairs={{0,3},{1,2},{2,1},{3,0},{4,7},{5,6},{6,5},{7,4},{8,11},{9,10},{10,... | collective-permute-start | bytes 1622024 | tf_op jit(solution)/shard_map/ppermute | solution.py:162
  96.9 13.9 %collective-permute-start.10 = (bf16[8,8,4224]{2,1,0:T(8,128)(2,1)S(1)}, bf16[8,8,4224]{2,1,0:T(8,128)(2,1)S(1)}, u32[]{:S(2)}, u32[]{:S(2)}) collective-permute-start(bf16[8,8,4224]{2,1,0:T(8,128)(2,1)S(1)} %collective-permute-done.9.refs_3_), channel_id=1, source_target_pairs={{0,12},{1,13},{2,14},{3,15},{4,8},{5,9},{6,10},{7,11},{8,4},{9,5},... | collective-permute-start | bytes 1622024 | tf_op jit(solution)/shard_map/ppermute | solution.py:162
  98.6 16.3 %collective-permute-start.25 = (bf16[8,8,4224]{2,1,0:T(8,128)(2,1)S(1)}, bf16[8,8,4224]{2,1,0:T(8,128)(2,1)S(1)}, u32[]{:S(2)}, u32[]{:S(2)}) collective-permute-start(bf16[8,8,4224]{2,1,0:T(8,128)(2,1)S(1)} %collective-permute-done.24.refs_6_), channel_id=1, source_target_pairs={{0,3},{1,2},{2,1},{3,0},{4,7},{5,6},{6,5},{7,4},{8,11},{9,10},{10,... | collective-permute-start | bytes 1622024 | tf_op jit(solution)/shard_map/ppermute | solution.py:162
  101.6 13.3 %collective-permute-start.21 = (bf16[8,8,4224]{2,1,0:T(8,128)(2,1)S(1)}, bf16[8,8,4224]{2,1,0:T(8,128)(2,1)S(1)}, u32[]{:S(2)}, u32[]{:S(2)}) collective-permute-start(bf16[8,8,4224]{2,1,0:T(8,128)(2,1)S(1)} %collective-permute-done.9.refs_3_), channel_id=1, source_target_pairs={{0,3},{1,2},{2,1},{3,0},{4,7},{5,6},{6,5},{7,4},{8,11},{9,10},{10,... | collective-permute-start | bytes 1622024 | tf_op jit(solution)/shard_map/ppermute | solution.py:162
  107.4 10.6 %collective-permute-start.17 = (bf16[8,8,4224]{2,1,0:T(8,128)(2,1)S(1)}, bf16[8,8,4224]{2,1,0:T(8,128)(2,1)S(1)}, u32[]{:S(2)}, u32[]{:S(2)}) collective-permute-start(bf16[8,8,4224]{2,1,0:T(8,128)(2,1)S(1)} %collective-permute-done.16.refs_11_), channel_id=1, source_target_pairs={{0,12},{1,13},{2,14},{3,15},{4,8},{5,9},{6,10},{7,11},{8,4},{9,5},... | collective-permute-start | bytes 1622024 | tf_op jit(solution)/shard_map/ppermute | solution.py:162
  109.2 10.6 %collective-permute-start.14 = (bf16[8,8,4224]{2,1,0:T(8,128)(2,1)S(1)}, bf16[8,8,4224]{2,1,0:T(8,128)(2,1)S(1)}, u32[]{:S(2)}, u32[]{:S(2)}) collective-permute-start(bf16[8,8,4224]{2,1,0:T(8,128)(2,1)S(1)} %collective-permute-done.13.refs_10_), channel_id=1, source_target_pairs={{0,48},{1,49},{2,50},{3,51},{4,52},{5,53},{6,54},{7,55},{8,56},{9,... | collective-permute-start | bytes 1622024 | tf_op jit(solution)/shard_map/ppermute | solution.py:162
  110.8 10.6 %collective-permute-start.11 = (bf16[8,8,4224]{2,1,0:T(8,128)(2,1)S(1)}, bf16[8,8,4224]{2,1,0:T(8,128)(2,1)S(1)}, u32[]{:S(2)}, u32[]{:S(2)}) collective-permute-start(bf16[8,8,4224]{2,1,0:T(8,128)(2,1)S(1)} %collective-permute-done.10.refs_9_), channel_id=1, source_target_pairs={{0,3},{1,2},{2,1},{3,0},{4,7},{5,6},{6,5},{7,4},{8,11},{9,10},{10,... | collective-permute-start | bytes 1622024 | tf_op jit(solution)/shard_map/ppermute | solution.py:162
where the time goes:
time: 123 us
  starting transfers between devices  45.2 us (37%)
  waiting for transfers between devices  44.3 us (36%)
  blocking collectives  20.2 us (16%)
  Pallas kernels  9.52 us (8%)
  between operations  2.06 us (2%)
  local copies, waits for them, and re-layouts  1.28 us (1%)
    ppermute x30, starting transfers between devices, permute(): return lax.ppermute(value, AXES, pairs)  45.2 us
    ppermute x30, waiting for transfers between devices, permute(): return lax.ppermute(value, AXES, pairs)  44.3 us
    all_to_all x1, blocking collectives, per_device(): sums = lax.all_to_all(own, AXES, 0, 0, tiled=True)  20.2 us
    pallas_call x3, Pallas kernels, per_device(): pl.pallas_call(functools.partial(place_kernel, which), in_specs=[anywhere...  6.54 us
    pallas_call x1, Pallas kernels, per_device(): pl.pallas_call(adam_kernel, in_specs=[vmem] * 6, out_specs=[vmem] * 6, ou...  2.91 us
  transfers between devices with their start and end apart: 30, of which 15 were waited for; matrix products, arithmetic and copies ran while one was open for 0% of the time, Pallas kernels for 4%

commit v1 on v0

--- a/solution.py
+++ b/solution.py
@@ -48,13 +48,8 @@
 
 
 def squares_kernel(
-    max_norm_ref, step_ref, gradient_ref, sums_ref, known_ref
+    gradient_ref, sums_ref
 ):
-    counted = jnp.full((1, LANES), step_ref[0].astype(jnp.float32))
-    known_ref[0:1, :] = jnp.full((1, LANES), max_norm_ref[0], jnp.float32)
-    known_ref[1:2, :] = 1.0 / (1.0 - jnp.exp(counted * log_first))
-    known_ref[2:3, :] = 1.0 / (1.0 - jnp.exp(counted * log_second))
-    known_ref[3:, :] = jnp.zeros((known_ref.shape[0] - 3, LANES), jnp.float32)
     rows, cols = gradient_ref.shape
     total = jnp.zeros((rows, LANES), jnp.float32)
     for at in range(0, cols, LANES):
@@ -65,16 +60,17 @@
 
 
 def adam_kernel(
-    sums_ref, known_ref, master_ref, gradient_ref, first_ref, second_ref,
+    max_norm_ref, step_ref, sums_ref, master_ref, gradient_ref, first_ref, second_ref,
     new_master_ref, new_first_ref, new_second_ref, top_ref, low_ref, one_ref,
 ):
     rows, cols = master_ref.shape
     line = jnp.sum(sums_ref[...], axis=0, keepdims=True)
     squares = jnp.sum(line, axis=1, keepdims=True)
-    norm_limit = known_ref[0:1, :]
+    norm_limit = jnp.full((1, LANES), max_norm_ref[0], jnp.float32)
+    counted = jnp.full((1, LANES), step_ref[0].astype(jnp.float32))
     clip_factor = norm_limit / jnp.maximum(jnp.sqrt(squares), norm_limit)
-    first_fix = known_ref[1:2, :]
-    second_fix = known_ref[2:3, :]
+    first_fix = 1.0 / (1.0 - jnp.exp(counted * log_first))
+    second_fix = 1.0 / (1.0 - jnp.exp(counted * log_second))
 
     lane = lax.broadcasted_iota(jnp.int32, (rows, LANES), 1)
     last_of_block = lane % BLOCK == BLOCK - 1
@@ -219,23 +215,23 @@
     vmem = pl.BlockSpec(memory_space=pltpu.VMEM)
     smem = pl.BlockSpec(memory_space=pltpu.SMEM)
     anywhere = pl.BlockSpec(memory_space=pl.ANY)
-    own, known = pl.pallas_call(
+    own = pl.pallas_call(
         squares_kernel,
-        in_specs=[smem, smem, vmem],
-        out_specs=[vmem] * 2,
-        out_shape=[jax.ShapeDtypeStruct((devices, LANES), f32), jax.ShapeDtypeStruct((8, LANES), f32)],
-        compiler_params=pltpu.CompilerParams(vmem_limit_bytes=2 << 20),
-    )(max_norm, step_count, gradient)
+        in_specs=[vmem],
+        out_specs=vmem,
+        out_shape=jax.ShapeDtypeStruct((devices, LANES), f32),
+        compiler_params=pltpu.CompilerParams(vmem_limit_bytes=54900 << 10),
+    )(gradient)
     sums = lax.all_to_all(own, AXES, 0, 0, tiled=True)
 
     half = jax.ShapeDtypeStruct((rows // 2, cols + LANES), jnp.bfloat16)
     new_master, new_first, new_second, top, low, first = pl.pallas_call(
         adam_kernel,
-        in_specs=[vmem] * 6,
+        in_specs=[smem, smem] + [vmem] * 5,
         out_specs=[vmem] * 6,
         out_shape=[state] * 3 + [half] * 3,
         compiler_params=pltpu.CompilerParams(vmem_limit_bytes=54600 << 10),
-    )(sums, known, master, gradient, first_moment, second_moment)
+    )(max_norm, step_count, sums, master, gradient, first_moment, second_moment)
 
     pieces = gather_pieces(redistribute(top, low, first))
     groups = rows * RING**3 // 2 // 8

time: 123 us -> 122 us (level)
  blocking collectives: 20.2 us -> 0 us
  starting transfers between devices: 45.2 us -> 56.4 us
  waiting for transfers between devices: 44.3 us -> 52.1 us
  Pallas kernels: 9.52 us -> 11.1 us
    all_to_all x1 -> x0, blocking collectives: 20.2 us -> none  [per_device(): sums = lax.all_to_all(own, AXES, 0, 0, tiled=True)]
    all_to_all x0 -> x1, starting transfers between devices: none -> 11.2 us  [per_device(): sums = lax.all_to_all(own, AXES, 0, 0, tiled=True)]
    all_to_all x0 -> x1, waiting for transfers between devices: none -> 7.84 us  [per_device(): sums = lax.all_to_all(own, AXES, 0, 0, tiled=True)]
    pallas_call x2, Pallas kernels: 2.95 us -> 4.57 us  [the longest x1 2.91 us: per_device(): pl.pallas_call(adam_kernel, in_specs=[smem, smem] + [vmem] * 5, out_specs...]
  transfers between devices with their start and end apart: 30 -> 31, of which waited for: 15 -> 16; matrix products, arithmetic and copies ran while one was open for 0% -> 0% of each run, Pallas kernels for 4% -> 4%
where the time goes in v1:
time: 122 us
  starting transfers between devices  56.4 us (46%)
  waiting for transfers between devices  52.1 us (43%)
  Pallas kernels  11.1 us (9%)
  between operations  2.06 us (2%)
    ppermute x30, starting transfers between devices, permute(): return lax.ppermute(value, AXES, pairs)  45.2 us
    ppermute x30, waiting for transfers between devices, permute(): return lax.ppermute(value, AXES, pairs)  44.3 us
    all_to_all x1, starting transfers between devices, per_device(): sums = lax.all_to_all(own, AXES, 0, 0, tiled=True)  11.2 us
    all_to_all x1, waiting for transfers between devices, per_device(): sums = lax.all_to_all(own, AXES, 0, 0, tiled=True)  7.84 us
    pallas_call x3, Pallas kernels, per_device(): pl.pallas_call(functools.partial(place_kernel, which), in_specs=[anywhere...  6.54 us
    pallas_call x1, Pallas kernels, per_device(): pl.pallas_call(adam_kernel, in_specs=[smem, smem] + [vmem] * 5, out_specs...  2.91 us
  transfers between devices with their start and end apart: 31, of which 16 were waited for; matrix products, arithmetic and copies ran while one was open for 0% of the time, Pallas kernels for 4%

profile of v1, /device:TPU:0, one launch (start us, length us, event | category | flops | bytes accessed | tf_op | source)
XLA Modules:
  0.0 122.0 jit_solution(11169192369090782159)
XLA Ops:
  0.6 1.7 %shard_map.101 = f32[128,128]{1,0:T(8,128)} custom-call(f32[48,2048]{1,0:T(8,128)} %gradient_ref.3), custom_call_target="tpu_custom_call" | custom-call | tf_op jit(solution)/shard_map/pallas_call | solution.py:218
  2.3 11.2 %all-to-all-start = ((f32[128,1,128]{2,1,0:T(1,128)}), f32[128,1,128]{2,1,0:T(1,128)S(1)}, u32[]{:S(2)}, u32[]{:S(2)}) async-start(f32[128,1,128]{2,1,0:T(1,128)} %bitcast.1), calls=%async_computation | async-start | bytes 131072 | tf_op jit(solution)/shard_map/all_to_all | solution.py:225
  14.8 7.8 %all-to-all-done = f32[128,1,128]{2,1,0:T(1,128)S(1)} async-done(((f32[128,1,128]{2,1,0:T(1,128)}), f32[128,1,128]{2,1,0:T(1,128)S(1)}, u32[]{:S(2)}, u32[]{:S(2)}) %all-to-all-start) | async-done | bytes 65568 | tf_op jit(solution)/shard_map/all_to_all | solution.py:225
  22.6 2.9 %shard_map.102 = (f32[48,2048]{1,0:T(8,128)}, f32[48,2048]{1,0:T(8,128)}, f32[48,2048]{1,0:T(8,128)}, bf16[24,2176]{1,0:T(8,128)(2,1)S(1)}, bf16[24,2176]{1,0:T(8,128)(2,1)S(1)}, /*index=5*/bf16[24,2176]{1,0:T(8,128)(2,1)S(1)}) custom-call(f32[1]{0:T(128)S(6)} %copy.27.max_norm_ref, s32[1]{0:T(128)S(6)} %copy.28.step_ref, f32[128,128]{1,0:T(8,128)S(1)} %bitcast.22, ...), custom_call_target="tpu_custom_call" | custom-call | tf_op jit(solution)/shard_map/pallas_call | solution.py:228
  25.5 0.9 collective-permute-start
  26.4 0.7 collective-permute-start.1
  27.1 1.6 %collective-permute-done.one_ref = bf16[24,2176]{1,0:T(8,128)(2,1)S(1)} collective-permute-done((bf16[24,2176]{1,0:T(8,128)(2,1)S(1)}, bf16[24,2176]{1,0:T(8,128)(2,1)S(1)}, u32[]{:S(2)}, u32[]{:S(2)}) %collective-permute-start) | collective-permute-done | bytes 104480 | tf_op jit(solution)/shard_map/ppermute | solution.py:158
  28.7 0.8 collective-permute-start.8
  29.5 2.3 %collective-permute-start.7 = (bf16[24,4224]{1,0:T(8,128)(2,1)S(1)}, bf16[24,4224]{1,0:T(8,128)(2,1)S(1)}, u32[]{:S(2)}, u32[]{:S(2)}) collective-permute-start(bf16[24,4224]{1,0:T(8,128)(2,1)S(1)} %shard_map.103), channel_id=1, source_target_pairs={{0,5},{1,4},{2,7},{3,6},{4,1},{5,0},{6,3},{7,2},{8,13},{9,12},{10,... | collective-permute-start | bytes 608264 | tf_op jit(solution)/shard_map/ppermute | solution.py:158
  31.7 1.4 %collective-permute-start.6 = (bf16[24,4224]{1,0:T(8,128)(2,1)S(1)}, bf16[24,4224]{1,0:T(8,128)(2,1)S(1)}, u32[]{:S(2)}, u32[]{:S(2)}) collective-permute-start(bf16[24,4224]{1,0:T(8,128)(2,1)S(1)} %shard_map.103), channel_id=1, source_target_pairs={{0,17},{1,16},{2,19},{3,18},{4,21},{5,20},{6,23},{7,22},{8,25},{9,... | collective-permute-start | bytes 608264 | tf_op jit(solution)/shard_map/ppermute | solution.py:158
  33.2 1.4 %collective-permute-start.5 = (bf16[24,4224]{1,0:T(8,128)(2,1)S(1)}, bf16[24,4224]{1,0:T(8,128)(2,1)S(1)}, u32[]{:S(2)}, u32[]{:S(2)}) collective-permute-start(bf16[24,4224]{1,0:T(8,128)(2,1)S(1)} %shard_map.103), channel_id=1, source_target_pairs={{0,1},{1,0},{2,3},{3,2},{4,5},{5,4},{6,7},{7,6},{8,9},{9,8},{10,11... | collective-permute-start | bytes 608264 | tf_op jit(solution)/shard_map/ppermute | solution.py:158
  34.6 0.6 collective-permute-start.2
  35.3 6.8 %collective-permute-done.2 = bf16[24,4224]{1,0:T(8,128)(2,1)S(1)} collective-permute-done((bf16[24,4224]{1,0:T(8,128)(2,1)S(1)}, bf16[24,4224]{1,0:T(8,128)(2,1)S(1)}, u32[]{:S(2)}, u32[]{:S(2)}) %collective-permute-start.2) | collective-permute-done | bytes 202784 | tf_op jit(solution)/shard_map/ppermute | solution.py:158
  42.0 1.2 collective-permute-start.3
  43.2 4.5 %collective-permute-done.3 = bf16[24,4224]{1,0:T(8,128)(2,1)S(1)} collective-permute-done((bf16[24,4224]{1,0:T(8,128)(2,1)S(1)}, bf16[24,4224]{1,0:T(8,128)(2,1)S(1)}, u32[]{:S(2)}, u32[]{:S(2)}) %collective-permute-start.3) | collective-permute-done | bytes 202784 | tf_op jit(solution)/shard_map/ppermute | solution.py:158
  47.7 1.2 collective-permute-start.4
  49.0 5.4 %collective-permute-done.4 = bf16[24,4224]{1,0:T(8,128)(2,1)S(1)} collective-permute-done((bf16[24,4224]{1,0:T(8,128)(2,1)S(1)}, bf16[24,4224]{1,0:T(8,128)(2,1)S(1)}, u32[]{:S(2)}, u32[]{:S(2)}) %collective-permute-start.4) | collective-permute-done | bytes 202784 | tf_op jit(solution)/shard_map/ppermute | solution.py:158
  54.7 5.0 %collective-permute-start.28 = (bf16[8,8,4224]{2,1,0:T(8,128)(2,1)S(1)}, bf16[8,8,4224]{2,1,0:T(8,128)(2,1)S(1)}, u32[]{:S(2)}, u32[]{:S(2)}) collective-permute-start(bf16[8,8,4224]{2,1,0:T(8,128)(2,1)S(1)} %get-tuple-element.29.refs_2_), channel_id=1, source_target_pairs={{0,48},{1,49},{2,50},{3,51},{4,52},{5,53},{6,54},{7,55},{8,56},{9,... | collective-permute-start | bytes 1622024 | tf_op jit(solution)/shard_map/ppermute | solution.py:158
  59.7 1.3 %collective-permute-start.20 = (bf16[8,8,4224]{2,1,0:T(8,128)(2,1)S(1)}, bf16[8,8,4224]{2,1,0:T(8,128)(2,1)S(1)}, u32[]{:S(2)}, u32[]{:S(2)}) collective-permute-start(bf16[8,8,4224]{2,1,0:T(8,128)(2,1)S(1)} %get-tuple-element.29.refs_2_), channel_id=1, source_target_pairs={{0,12},{1,13},{2,14},{3,15},{4,8},{5,9},{6,10},{7,11},{8,4},{9,5},... | collective-permute-start | bytes 1622024 | tf_op jit(solution)/shard_map/ppermute | solution.py:158
  61.0 0.9 collective-permute-start.15
  61.8 2.4 %collective-permute-start.26 = (bf16[8,8,4224]{2,1,0:T(8,128)(2,1)S(1)}, bf16[8,8,4224]{2,1,0:T(8,128)(2,1)S(1)}, u32[]{:S(2)}, u32[]{:S(2)}) collective-permute-start(bf16[8,8,4224]{2,1,0:T(8,128)(2,1)S(1)} %get-tuple-element.30.refs_1_), channel_id=1, source_target_pairs={{0,3},{1,2},{2,1},{3,0},{4,7},{5,6},{6,5},{7,4},{8,11},{9,10},{10,... | collective-permute-start | bytes 1622024 | tf_op jit(solution)/shard_map/ppermute | solution.py:158
  64.3 4.1 %collective-permute-done.28.refs_8_ = bf16[8,8,4224]{2,1,0:T(8,128)(2,1)S(1)} collective-permute-done((bf16[8,8,4224]{2,1,0:T(8,128)(2,1)S(1)}, bf16[8,8,4224]{2,1,0:T(8,128)(2,1)S(1)}, u32[]{:S(2)}, u32[]{:S(2)}) %collective-permute-start.28) | collective-permute-done | bytes 540704 | tf_op jit(solution)/shard_map/ppermute | solution.py:158
  68.4 1.7 %collective-permute-start.12 = (bf16[8,8,4224]{2,1,0:T(8,128)(2,1)S(1)}, bf16[8,8,4224]{2,1,0:T(8,128)(2,1)S(1)}, u32[]{:S(2)}, u32[]{:S(2)}) collective-permute-start(bf16[8,8,4224]{2,1,0:T(8,128)(2,1)S(1)} %get-tuple-element.30.refs_1_), channel_id=1, source_target_pairs={{0,12},{1,13},{2,14},{3,15},{4,8},{5,9},{6,10},{7,11},{8,4},{9,5},... | collective-permute-start | bytes 1622024 | tf_op jit(solution)/shard_map/ppermute | solution.py:158
  70.2 1.4 %collective-permute-start.24 = (bf16[8,8,4224]{2,1,0:T(8,128)(2,1)S(1)}, bf16[8,8,4224]{2,1,0:T(8,128)(2,1)S(1)}, u32[]{:S(2)}, u32[]{:S(2)}) collective-permute-start(bf16[8,8,4224]{2,1,0:T(8,128)(2,1)S(1)} %get-tuple-element.31.refs_0_), channel_id=1, source_target_pairs={{0,12},{1,13},{2,14},{3,15},{4,8},{5,9},{6,10},{7,11},{8,4},{9,5},... | collective-permute-start | bytes 1622024 | tf_op jit(solution)/shard_map/ppermute | solution.py:158
  71.6 1.9 %collective-permute-start.18 = (bf16[8,8,4224]{2,1,0:T(8,128)(2,1)S(1)}, bf16[8,8,4224]{2,1,0:T(8,128)(2,1)S(1)}, u32[]{:S(2)}, u32[]{:S(2)}) collective-permute-start(bf16[8,8,4224]{2,1,0:T(8,128)(2,1)S(1)} %get-tuple-element.31.refs_0_), channel_id=1, source_target_pairs={{0,3},{1,2},{2,1},{3,0},{4,7},{5,6},{6,5},{7,4},{8,11},{9,10},{10,... | collective-permute-start | bytes 1622024 | tf_op jit(solution)/shard_map/ppermute | solution.py:158
  73.6 3.8 %collective-permute-done.26.refs_7_ = bf16[8,8,4224]{2,1,0:T(8,128)(2,1)S(1)} collective-permute-done((bf16[8,8,4224]{2,1,0:T(8,128)(2,1)S(1)}, bf16[8,8,4224]{2,1,0:T(8,128)(2,1)S(1)}, u32[]{:S(2)}, u32[]{:S(2)}) %collective-permute-start.26) | collective-permute-done | bytes 540704 | tf_op jit(solution)/shard_map/ppermute | solution.py:158
  77.4 2.0 %collective-permute-start.29 = (bf16[8,8,4224]{2,1,0:T(8,128)(2,1)S(1)}, bf16[8,8,4224]{2,1,0:T(8,128)(2,1)S(1)}, u32[]{:S(2)}, u32[]{:S(2)}) collective-permute-start(bf16[8,8,4224]{2,1,0:T(8,128)(2,1)S(1)} %collective-permute-done.28.refs_8_), channel_id=1, source_target_pairs={{0,12},{1,13},{2,14},{3,15},{4,8},{5,9},{6,10},{7,11},{8,4},{9,5},... | collective-permute-start | bytes 1622024 | tf_op jit(solution)/shard_map/ppermute | solution.py:158
  79.4 1.3 %collective-permute-start.23 = (bf16[8,8,4224]{2,1,0:T(8,128)(2,1)S(1)}, bf16[8,8,4224]{2,1,0:T(8,128)(2,1)S(1)}, u32[]{:S(2)}, u32[]{:S(2)}) collective-permute-start(bf16[8,8,4224]{2,1,0:T(8,128)(2,1)S(1)} %collective-permute-done.15.refs_5_), channel_id=1, source_target_pairs={{0,12},{1,13},{2,14},{3,15},{4,8},{5,9},{6,10},{7,11},{8,4},{9,5},... | collective-permute-start | bytes 1622024 | tf_op jit(solution)/shard_map/ppermute | solution.py:158
  80.7 4.1 %collective-permute-done.24.refs_6_ = bf16[8,8,4224]{2,1,0:T(8,128)(2,1)S(1)} collective-permute-done((bf16[8,8,4224]{2,1,0:T(8,128)(2,1)S(1)}, bf16[8,8,4224]{2,1,0:T(8,128)(2,1)S(1)}, u32[]{:S(2)}, u32[]{:S(2)}) %collective-permute-start.24) | collective-permute-done | bytes 540704 | tf_op jit(solution)/shard_map/ppermute | solution.py:158
  84.7 2.2 %collective-permute-start.16 = (bf16[8,8,4224]{2,1,0:T(8,128)(2,1)S(1)}, bf16[8,8,4224]{2,1,0:T(8,128)(2,1)S(1)}, u32[]{:S(2)}, u32[]{:S(2)}) collective-permute-start(bf16[8,8,4224]{2,1,0:T(8,128)(2,1)S(1)} %collective-permute-done.15.refs_5_), channel_id=1, source_target_pairs={{0,48},{1,49},{2,50},{3,51},{4,52},{5,53},{6,54},{7,55},{8,56},{9,... | collective-permute-start | bytes 1622024 | tf_op jit(solution)/shard_map/ppermute | solution.py:158
  86.9 1.1 collective-permute-start.27
  88.0 2.2 %collective-permute-start.22 = (bf16[8,8,4224]{2,1,0:T(8,128)(2,1)S(1)}, bf16[8,8,4224]{2,1,0:T(8,128)(2,1)S(1)}, u32[]{:S(2)}, u32[]{:S(2)}) collective-permute-start(bf16[8,8,4224]{2,1,0:T(8,128)(2,1)S(1)} %collective-permute-done.12.refs_4_), channel_id=1, source_target_pairs={{0,48},{1,49},{2,50},{3,51},{4,52},{5,53},{6,54},{7,55},{8,56},{9,... | collective-permute-start | bytes 1622024 | tf_op jit(solution)/shard_map/ppermute | solution.py:158
  90.5 1.9 %collective-permute-start.13 = (bf16[8,8,4224]{2,1,0:T(8,128)(2,1)S(1)}, bf16[8,8,4224]{2,1,0:T(8,128)(2,1)S(1)}, u32[]{:S(2)}, u32[]{:S(2)}) collective-permute-start(bf16[8,8,4224]{2,1,0:T(8,128)(2,1)S(1)} %collective-permute-done.12.refs_4_), channel_id=1, source_target_pairs={{0,3},{1,2},{2,1},{3,0},{4,7},{5,6},{6,5},{7,4},{8,11},{9,10},{10,... | collective-permute-start | bytes 1622024 | tf_op jit(solution)/shard_map/ppermute | solution.py:158
  92.5 3.8 %collective-permute-done.23.refs_5_ = bf16[8,8,4224]{2,1,0:T(8,128)(2,1)S(1)} collective-permute-done((bf16[8,8,4224]{2,1,0:T(8,128)(2,1)S(1)}, bf16[8,8,4224]{2,1,0:T(8,128)(2,1)S(1)}, u32[]{:S(2)}, u32[]{:S(2)}) %collective-permute-start.23) | collective-permute-done | bytes 540704 | tf_op jit(solution)/shard_map/ppermute | solution.py:158
  96.3 1.7 %collective-permute-start.10 = (bf16[8,8,4224]{2,1,0:T(8,128)(2,1)S(1)}, bf16[8,8,4224]{2,1,0:T(8,128)(2,1)S(1)}, u32[]{:S(2)}, u32[]{:S(2)}) collective-permute-start(bf16[8,8,4224]{2,1,0:T(8,128)(2,1)S(1)} %collective-permute-done.9.refs_3_), channel_id=1, source_target_pairs={{0,12},{1,13},{2,14},{3,15},{4,8},{5,9},{6,10},{7,11},{8,4},{9,5},... | collective-permute-start | bytes 1622024 | tf_op jit(solution)/shard_map/ppermute | solution.py:158
  98.0 1.2 %collective-permute-start.25 = (bf16[8,8,4224]{2,1,0:T(8,128)(2,1)S(1)}, bf16[8,8,4224]{2,1,0:T(8,128)(2,1)S(1)}, u32[]{:S(2)}, u32[]{:S(2)}) collective-permute-start(bf16[8,8,4224]{2,1,0:T(8,128)(2,1)S(1)} %collective-permute-done.24.refs_6_), channel_id=1, source_target_pairs={{0,3},{1,2},{2,1},{3,0},{4,7},{5,6},{6,5},{7,4},{8,11},{9,10},{10,... | collective-permute-start | bytes 1622024 | tf_op jit(solution)/shard_map/ppermute | solution.py:158
  99.3 1.8 %collective-permute-done.27.refs_7_ = bf16[8,8,4224]{2,1,0:T(8,128)(2,1)S(1)} collective-permute-done((bf16[8,8,4224]{2,1,0:T(8,128)(2,1)S(1)}, bf16[8,8,4224]{2,1,0:T(8,128)(2,1)S(1)}, u32[]{:S(2)}, u32[]{:S(2)}) %collective-permute-start.27) | collective-permute-done | bytes 540704 | tf_op jit(solution)/shard_map/ppermute | solution.py:158
  101.1 1.9 %collective-permute-start.21 = (bf16[8,8,4224]{2,1,0:T(8,128)(2,1)S(1)}, bf16[8,8,4224]{2,1,0:T(8,128)(2,1)S(1)}, u32[]{:S(2)}, u32[]{:S(2)}) collective-permute-start(bf16[8,8,4224]{2,1,0:T(8,128)(2,1)S(1)} %collective-permute-done.9.refs_3_), channel_id=1, source_target_pairs={{0,3},{1,2},{2,1},{3,0},{4,7},{5,6},{6,5},{7,4},{8,11},{9,10},{10,... | collective-permute-start | bytes 1622024 | tf_op jit(solution)/shard_map/ppermute | solution.py:158
  103.0 3.8 %collective-permute-done.22.refs_4_ = bf16[8,8,4224]{2,1,0:T(8,128)(2,1)S(1)} collective-permute-done((bf16[8,8,4224]{2,1,0:T(8,128)(2,1)S(1)}, bf16[8,8,4224]{2,1,0:T(8,128)(2,1)S(1)}, u32[]{:S(2)}, u32[]{:S(2)}) %collective-permute-start.22) | collective-permute-done | bytes 540704 | tf_op jit(solution)/shard_map/ppermute | solution.py:158
  106.9 1.7 %collective-permute-start.17 = (bf16[8,8,4224]{2,1,0:T(8,128)(2,1)S(1)}, bf16[8,8,4224]{2,1,0:T(8,128)(2,1)S(1)}, u32[]{:S(2)}, u32[]{:S(2)}) collective-permute-start(bf16[8,8,4224]{2,1,0:T(8,128)(2,1)S(1)} %collective-permute-done.16.refs_11_), channel_id=1, source_target_pairs={{0,12},{1,13},{2,14},{3,15},{4,8},{5,9},{6,10},{7,11},{8,4},{9,5},... | collective-permute-start | bytes 1622024 | tf_op jit(solution)/shard_map/ppermute | solution.py:158
  108.6 1.6 %collective-permute-start.14 = (bf16[8,8,4224]{2,1,0:T(8,128)(2,1)S(1)}, bf16[8,8,4224]{2,1,0:T(8,128)(2,1)S(1)}, u32[]{:S(2)}, u32[]{:S(2)}) collective-permute-start(bf16[8,8,4224]{2,1,0:T(8,128)(2,1)S(1)} %collective-permute-done.13.refs_10_), channel_id=1, source_target_pairs={{0,48},{1,49},{2,50},{3,51},{4,52},{5,53},{6,54},{7,55},{8,56},{9,... | collective-permute-start | bytes 1622024 | tf_op jit(solution)/shard_map/ppermute | solution.py:158
  110.2 1.2 collective-permute-start.11
  111.4 2.9 %shard_map.104 = (bf16[192,8,4096]{2,1,0:T(8,128)(2,1)}, bf16[192,8,128]{2,1,0:T(8,128)(2,1)}) custom-call(bf16[8,8,4224]{2,1,0:T(8,128)(2,1)S(1)} %get-tuple-element.31.refs_0_, bf16[8,8,4224]{2,1,0:T(8,128)(2,1)S(1)} %get-tuple-element.30.refs_1_, bf16[8,8,4224]{2,1,0:T(8,128)(2,1)S(1)} %get-tuple-element.29.refs_2_, ...), custom_call_target="tpu_custom_call" | custom-call | tf_op jit(solution)/shard_map/pallas_call | solution.py:241
  114.4 2.4 %shard_map.105 = (bf16[192,8,4096]{2,1,0:T(8,128)(2,1)}, bf16[192,8,128]{2,1,0:T(8,128)(2,1)}) custom-call(bf16[8,8,4224]{2,1,0:T(8,128)(2,1)S(1)} %collective-permute-done.18.refs_0_, bf16[8,8,4224]{2,1,0:T(8,128)(2,1)S(1)} %collective-permute-done.19.refs_1_, ...), custom_call_target="tpu_custom_call", output_to_operand_aliasing={{0}: (9, {}), {1}: (10, {})} | custom-call | tf_op jit(solution)/shard_map/pallas_call | solution.py:241
  116.8 0.6 collective-permute-done.17.refs_2_
  117.5 1.7 %collective-permute-done.14.refs_1_ = bf16[8,8,4224]{2,1,0:T(8,128)(2,1)S(1)} collective-permute-done((bf16[8,8,4224]{2,1,0:T(8,128)(2,1)S(1)}, bf16[8,8,4224]{2,1,0:T(8,128)(2,1)S(1)}, u32[]{:S(2)}, u32[]{:S(2)}) %collective-permute-start.14) | collective-permute-done | bytes 540704 | tf_op jit(solution)/shard_map/ppermute | solution.py:158
  119.2 1.6 %collective-permute-done.11.refs_0_ = bf16[8,8,4224]{2,1,0:T(8,128)(2,1)S(1)} collective-permute-done((bf16[8,8,4224]{2,1,0:T(8,128)(2,1)S(1)}, bf16[8,8,4224]{2,1,0:T(8,128)(2,1)S(1)}, u32[]{:S(2)}, u32[]{:S(2)}) %collective-permute-start.11) | collective-permute-done | bytes 540704 | tf_op jit(solution)/shard_map/ppermute | solution.py:158
  120.8 1.2 shard_map.106
  (29 shorter events, 1.1 us)
Async XLA Ops:
  2.3 20.3 %all-to-all-start = ((f32[128,1,128]{2,1,0:T(1,128)}), f32[128,1,128]{2,1,0:T(1,128)S(1)}, u32[]{:S(2)}, u32[]{:S(2)}) async-start(f32[128,1,128]{2,1,0:T(1,128)} %bitcast.1), calls=%async_computation | async-start | bytes 131072 | tf_op jit(solution)/shard_map/all_to_all | solution.py:225
  25.5 3.2 %collective-permute-start = (bf16[24,2176]{1,0:T(8,128)(2,1)S(1)}, bf16[24,2176]{1,0:T(8,128)(2,1)S(1)}, u32[]{:S(2)}, u32[]{:S(2)}) collective-permute-start(bf16[24,2176]{1,0:T(8,128)(2,1)S(1)} %get-tuple-element.21), channel_id=1, source_target_pairs={{0,48},{1,49},{2,50},{3,51},{4,52},{5,53},{6,54},{7,55},{8,56},{9,... | collective-permute-start | bytes 313352 | tf_op jit(solution)/shard_map/ppermute | solution.py:158
  26.4 2.3 %collective-permute-start.1 = (bf16[24,2176]{1,0:T(8,128)(2,1)S(1)}, bf16[24,2176]{1,0:T(8,128)(2,1)S(1)}, u32[]{:S(2)}, u32[]{:S(2)}) collective-permute-start(bf16[24,2176]{1,0:T(8,128)(2,1)S(1)} %get-tuple-element.22), channel_id=1, source_target_pairs={{32,80},{33,81},{34,82},{35,83},{36,84},{37,85},{38,86},{39,87},{4... | collective-permute-start | bytes 313352 | tf_op jit(solution)/shard_map/ppermute | solution.py:158
  28.7 25.8 %collective-permute-start.8 = (bf16[24,4224]{1,0:T(8,128)(2,1)S(1)}, bf16[24,4224]{1,0:T(8,128)(2,1)S(1)}, u32[]{:S(2)}, u32[]{:S(2)}) collective-permute-start(bf16[24,4224]{1,0:T(8,128)(2,1)S(1)} %shard_map.103), channel_id=1, source_target_pairs={{0,21},{1,20},{2,23},{3,22},{4,17},{5,16},{6,19},{7,18},{8,29},{9,... | collective-permute-start | bytes 608264 | tf_op jit(solution)/shard_map/ppermute | solution.py:158
  29.5 25.0 %collective-permute-start.7 = (bf16[24,4224]{1,0:T(8,128)(2,1)S(1)}, bf16[24,4224]{1,0:T(8,128)(2,1)S(1)}, u32[]{:S(2)}, u32[]{:S(2)}) collective-permute-start(bf16[24,4224]{1,0:T(8,128)(2,1)S(1)} %shard_map.103), channel_id=1, source_target_pairs={{0,5},{1,4},{2,7},{3,6},{4,1},{5,0},{6,3},{7,2},{8,13},{9,12},{10,... | collective-permute-start | bytes 608264 | tf_op jit(solution)/shard_map/ppermute | solution.py:158
  31.7 22.7 %collective-permute-start.6 = (bf16[24,4224]{1,0:T(8,128)(2,1)S(1)}, bf16[24,4224]{1,0:T(8,128)(2,1)S(1)}, u32[]{:S(2)}, u32[]{:S(2)}) collective-permute-start(bf16[24,4224]{1,0:T(8,128)(2,1)S(1)} %shard_map.103), channel_id=1, source_target_pairs={{0,17},{1,16},{2,19},{3,18},{4,21},{5,20},{6,23},{7,22},{8,25},{9,... | collective-permute-start | bytes 608264 | tf_op jit(solution)/shard_map/ppermute | solution.py:158
  33.2 21.2 %collective-permute-start.5 = (bf16[24,4224]{1,0:T(8,128)(2,1)S(1)}, bf16[24,4224]{1,0:T(8,128)(2,1)S(1)}, u32[]{:S(2)}, u32[]{:S(2)}) collective-permute-start(bf16[24,4224]{1,0:T(8,128)(2,1)S(1)} %shard_map.103), channel_id=1, source_target_pairs={{0,1},{1,0},{2,3},{3,2},{4,5},{5,4},{6,7},{7,6},{8,9},{9,8},{10,11... | collective-permute-start | bytes 608264 | tf_op jit(solution)/shard_map/ppermute | solution.py:158
  34.6 7.4 %collective-permute-start.2 = (bf16[24,4224]{1,0:T(8,128)(2,1)S(1)}, bf16[24,4224]{1,0:T(8,128)(2,1)S(1)}, u32[]{:S(2)}, u32[]{:S(2)}) collective-permute-start(bf16[24,4224]{1,0:T(8,128)(2,1)S(1)} %shard_map.103), channel_id=1, source_target_pairs={{0,16},{1,17},{2,18},{3,19},{4,20},{5,21},{6,22},{7,23},{8,24},{9,... | collective-permute-start | bytes 608264 | tf_op jit(solution)/shard_map/ppermute | solution.py:158
  42.0 5.7 %collective-permute-start.3 = (bf16[24,4224]{1,0:T(8,128)(2,1)S(1)}, bf16[24,4224]{1,0:T(8,128)(2,1)S(1)}, u32[]{:S(2)}, u32[]{:S(2)}) collective-permute-start(bf16[24,4224]{1,0:T(8,128)(2,1)S(1)} %shard_map.103), channel_id=1, source_target_pairs={{0,4},{1,5},{2,6},{3,7},{4,0},{5,1},{6,2},{7,3},{8,12},{9,13},{10,... | collective-permute-start | bytes 608264 | tf_op jit(solution)/shard_map/ppermute | solution.py:158
  47.7 6.6 %collective-permute-start.4 = (bf16[24,4224]{1,0:T(8,128)(2,1)S(1)}, bf16[24,4224]{1,0:T(8,128)(2,1)S(1)}, u32[]{:S(2)}, u32[]{:S(2)}) collective-permute-start(bf16[24,4224]{1,0:T(8,128)(2,1)S(1)} %shard_map.103), channel_id=1, source_target_pairs={{0,20},{1,21},{2,22},{3,23},{4,16},{5,17},{6,18},{7,19},{8,28},{9,... | collective-permute-start | bytes 608264 | tf_op jit(solution)/shard_map/ppermute | solution.py:158
  54.7 13.7 %collective-permute-start.28 = (bf16[8,8,4224]{2,1,0:T(8,128)(2,1)S(1)}, bf16[8,8,4224]{2,1,0:T(8,128)(2,1)S(1)}, u32[]{:S(2)}, u32[]{:S(2)}) collective-permute-start(bf16[8,8,4224]{2,1,0:T(8,128)(2,1)S(1)} %get-tuple-element.29.refs_2_), channel_id=1, source_target_pairs={{0,48},{1,49},{2,50},{3,51},{4,52},{5,53},{6,54},{7,55},{8,56},{9,... | collective-permute-start | bytes 1622024 | tf_op jit(solution)/shard_map/ppermute | solution.py:158
  59.7 10.6 %collective-permute-start.20 = (bf16[8,8,4224]{2,1,0:T(8,128)(2,1)S(1)}, bf16[8,8,4224]{2,1,0:T(8,128)(2,1)S(1)}, u32[]{:S(2)}, u32[]{:S(2)}) collective-permute-start(bf16[8,8,4224]{2,1,0:T(8,128)(2,1)S(1)} %get-tuple-element.29.refs_2_), channel_id=1, source_target_pairs={{0,12},{1,13},{2,14},{3,15},{4,8},{5,9},{6,10},{7,11},{8,4},{9,5},... | collective-permute-start | bytes 1622024 | tf_op jit(solution)/shard_map/ppermute | solution.py:158
  61.0 10.7 %collective-permute-start.15 = (bf16[8,8,4224]{2,1,0:T(8,128)(2,1)S(1)}, bf16[8,8,4224]{2,1,0:T(8,128)(2,1)S(1)}, u32[]{:S(2)}, u32[]{:S(2)}) collective-permute-start(bf16[8,8,4224]{2,1,0:T(8,128)(2,1)S(1)} %get-tuple-element.29.refs_2_), channel_id=1, source_target_pairs={{0,3},{1,2},{2,1},{3,0},{4,7},{5,6},{6,5},{7,4},{8,11},{9,10},{10,... | collective-permute-start | bytes 1622024 | tf_op jit(solution)/shard_map/ppermute | solution.py:158
  61.8 15.5 %collective-permute-start.26 = (bf16[8,8,4224]{2,1,0:T(8,128)(2,1)S(1)}, bf16[8,8,4224]{2,1,0:T(8,128)(2,1)S(1)}, u32[]{:S(2)}, u32[]{:S(2)}) collective-permute-start(bf16[8,8,4224]{2,1,0:T(8,128)(2,1)S(1)} %get-tuple-element.30.refs_1_), channel_id=1, source_target_pairs={{0,3},{1,2},{2,1},{3,0},{4,7},{5,6},{6,5},{7,4},{8,11},{9,10},{10,... | collective-permute-start | bytes 1622024 | tf_op jit(solution)/shard_map/ppermute | solution.py:158
  64.2 13.2 %collective-permute-start.19 = (bf16[8,8,4224]{2,1,0:T(8,128)(2,1)S(1)}, bf16[8,8,4224]{2,1,0:T(8,128)(2,1)S(1)}, u32[]{:S(2)}, u32[]{:S(2)}) collective-permute-start(bf16[8,8,4224]{2,1,0:T(8,128)(2,1)S(1)} %get-tuple-element.30.refs_1_), channel_id=1, source_target_pairs={{0,48},{1,49},{2,50},{3,51},{4,52},{5,53},{6,54},{7,55},{8,56},{9,... | collective-permute-start | bytes 1622024 | tf_op jit(solution)/shard_map/ppermute | solution.py:158
  68.4 11.0 %collective-permute-start.12 = (bf16[8,8,4224]{2,1,0:T(8,128)(2,1)S(1)}, bf16[8,8,4224]{2,1,0:T(8,128)(2,1)S(1)}, u32[]{:S(2)}, u32[]{:S(2)}) collective-permute-start(bf16[8,8,4224]{2,1,0:T(8,128)(2,1)S(1)} %get-tuple-element.30.refs_1_), channel_id=1, source_target_pairs={{0,12},{1,13},{2,14},{3,15},{4,8},{5,9},{6,10},{7,11},{8,4},{9,5},... | collective-permute-start | bytes 1622024 | tf_op jit(solution)/shard_map/ppermute | solution.py:158
  70.2 14.5 %collective-permute-start.24 = (bf16[8,8,4224]{2,1,0:T(8,128)(2,1)S(1)}, bf16[8,8,4224]{2,1,0:T(8,128)(2,1)S(1)}, u32[]{:S(2)}, u32[]{:S(2)}) collective-permute-start(bf16[8,8,4224]{2,1,0:T(8,128)(2,1)S(1)} %get-tuple-element.31.refs_0_), channel_id=1, source_target_pairs={{0,12},{1,13},{2,14},{3,15},{4,8},{5,9},{6,10},{7,11},{8,4},{9,5},... | collective-permute-start | bytes 1622024 | tf_op jit(solution)/shard_map/ppermute | solution.py:158
  71.6 15.3 %collective-permute-start.18 = (bf16[8,8,4224]{2,1,0:T(8,128)(2,1)S(1)}, bf16[8,8,4224]{2,1,0:T(8,128)(2,1)S(1)}, u32[]{:S(2)}, u32[]{:S(2)}) collective-permute-start(bf16[8,8,4224]{2,1,0:T(8,128)(2,1)S(1)} %get-tuple-element.31.refs_0_), channel_id=1, source_target_pairs={{0,3},{1,2},{2,1},{3,0},{4,7},{5,6},{6,5},{7,4},{8,11},{9,10},{10,... | collective-permute-start | bytes 1622024 | tf_op jit(solution)/shard_map/ppermute | solution.py:158
  77.3 10.7 %collective-permute-start.9 = (bf16[8,8,4224]{2,1,0:T(8,128)(2,1)S(1)}, bf16[8,8,4224]{2,1,0:T(8,128)(2,1)S(1)}, u32[]{:S(2)}, u32[]{:S(2)}) collective-permute-start(bf16[8,8,4224]{2,1,0:T(8,128)(2,1)S(1)} %get-tuple-element.31.refs_0_), channel_id=1, source_target_pairs={{0,48},{1,49},{2,50},{3,51},{4,52},{5,53},{6,54},{7,55},{8,56},{9,... | collective-permute-start | bytes 1622024 | tf_op jit(solution)/shard_map/ppermute | solution.py:158
  77.4 13.1 %collective-permute-start.29 = (bf16[8,8,4224]{2,1,0:T(8,128)(2,1)S(1)}, bf16[8,8,4224]{2,1,0:T(8,128)(2,1)S(1)}, u32[]{:S(2)}, u32[]{:S(2)}) collective-permute-start(bf16[8,8,4224]{2,1,0:T(8,128)(2,1)S(1)} %collective-permute-done.28.refs_8_), channel_id=1, source_target_pairs={{0,12},{1,13},{2,14},{3,15},{4,8},{5,9},{6,10},{7,11},{8,4},{9,5},... | collective-permute-start | bytes 1622024 | tf_op jit(solution)/shard_map/ppermute | solution.py:158
  79.4 16.9 %collective-permute-start.23 = (bf16[8,8,4224]{2,1,0:T(8,128)(2,1)S(1)}, bf16[8,8,4224]{2,1,0:T(8,128)(2,1)S(1)}, u32[]{:S(2)}, u32[]{:S(2)}) collective-permute-start(bf16[8,8,4224]{2,1,0:T(8,128)(2,1)S(1)} %collective-permute-done.15.refs_5_), channel_id=1, source_target_pairs={{0,12},{1,13},{2,14},{3,15},{4,8},{5,9},{6,10},{7,11},{8,4},{9,5},... | collective-permute-start | bytes 1622024 | tf_op jit(solution)/shard_map/ppermute | solution.py:158
  84.7 13.3 %collective-permute-start.16 = (bf16[8,8,4224]{2,1,0:T(8,128)(2,1)S(1)}, bf16[8,8,4224]{2,1,0:T(8,128)(2,1)S(1)}, u32[]{:S(2)}, u32[]{:S(2)}) collective-permute-start(bf16[8,8,4224]{2,1,0:T(8,128)(2,1)S(1)} %collective-permute-done.15.refs_5_), channel_id=1, source_target_pairs={{0,48},{1,49},{2,50},{3,51},{4,52},{5,53},{6,54},{7,55},{8,56},{9,... | collective-permute-start | bytes 1622024 | tf_op jit(solution)/shard_map/ppermute | solution.py:158
  86.9 14.2 %collective-permute-start.27 = (bf16[8,8,4224]{2,1,0:T(8,128)(2,1)S(1)}, bf16[8,8,4224]{2,1,0:T(8,128)(2,1)S(1)}, u32[]{:S(2)}, u32[]{:S(2)}) collective-permute-start(bf16[8,8,4224]{2,1,0:T(8,128)(2,1)S(1)} %collective-permute-done.26.refs_7_), channel_id=1, source_target_pairs={{0,48},{1,49},{2,50},{3,51},{4,52},{5,53},{6,54},{7,55},{8,56},{9,... | collective-permute-start | bytes 1622024 | tf_op jit(solution)/shard_map/ppermute | solution.py:158
  88.0 18.9 %collective-permute-start.22 = (bf16[8,8,4224]{2,1,0:T(8,128)(2,1)S(1)}, bf16[8,8,4224]{2,1,0:T(8,128)(2,1)S(1)}, u32[]{:S(2)}, u32[]{:S(2)}) collective-permute-start(bf16[8,8,4224]{2,1,0:T(8,128)(2,1)S(1)} %collective-permute-done.12.refs_4_), channel_id=1, source_target_pairs={{0,48},{1,49},{2,50},{3,51},{4,52},{5,53},{6,54},{7,55},{8,56},{9,... | collective-permute-start | bytes 1622024 | tf_op jit(solution)/shard_map/ppermute | solution.py:158
  90.5 18.1 %collective-permute-start.13 = (bf16[8,8,4224]{2,1,0:T(8,128)(2,1)S(1)}, bf16[8,8,4224]{2,1,0:T(8,128)(2,1)S(1)}, u32[]{:S(2)}, u32[]{:S(2)}) collective-permute-start(bf16[8,8,4224]{2,1,0:T(8,128)(2,1)S(1)} %collective-permute-done.12.refs_4_), channel_id=1, source_target_pairs={{0,3},{1,2},{2,1},{3,0},{4,7},{5,6},{6,5},{7,4},{8,11},{9,10},{10,... | collective-permute-start | bytes 1622024 | tf_op jit(solution)/shard_map/ppermute | solution.py:158
  96.3 13.9 %collective-permute-start.10 = (bf16[8,8,4224]{2,1,0:T(8,128)(2,1)S(1)}, bf16[8,8,4224]{2,1,0:T(8,128)(2,1)S(1)}, u32[]{:S(2)}, u32[]{:S(2)}) collective-permute-start(bf16[8,8,4224]{2,1,0:T(8,128)(2,1)S(1)} %collective-permute-done.9.refs_3_), channel_id=1, source_target_pairs={{0,12},{1,13},{2,14},{3,15},{4,8},{5,9},{6,10},{7,11},{8,4},{9,5},... | collective-permute-start | bytes 1622024 | tf_op jit(solution)/shard_map/ppermute | solution.py:158
  98.0 16.3 %collective-permute-start.25 = (bf16[8,8,4224]{2,1,0:T(8,128)(2,1)S(1)}, bf16[8,8,4224]{2,1,0:T(8,128)(2,1)S(1)}, u32[]{:S(2)}, u32[]{:S(2)}) collective-permute-start(bf16[8,8,4224]{2,1,0:T(8,128)(2,1)S(1)} %collective-permute-done.24.refs_6_), channel_id=1, source_target_pairs={{0,3},{1,2},{2,1},{3,0},{4,7},{5,6},{6,5},{7,4},{8,11},{9,10},{10,... | collective-permute-start | bytes 1622024 | tf_op jit(solution)/shard_map/ppermute | solution.py:158
  101.1 13.3 %collective-permute-start.21 = (bf16[8,8,4224]{2,1,0:T(8,128)(2,1)S(1)}, bf16[8,8,4224]{2,1,0:T(8,128)(2,1)S(1)}, u32[]{:S(2)}, u32[]{:S(2)}) collective-permute-start(bf16[8,8,4224]{2,1,0:T(8,128)(2,1)S(1)} %collective-permute-done.9.refs_3_), channel_id=1, source_target_pairs={{0,3},{1,2},{2,1},{3,0},{4,7},{5,6},{6,5},{7,4},{8,11},{9,10},{10,... | collective-permute-start | bytes 1622024 | tf_op jit(solution)/shard_map/ppermute | solution.py:158
  106.9 10.6 %collective-permute-start.17 = (bf16[8,8,4224]{2,1,0:T(8,128)(2,1)S(1)}, bf16[8,8,4224]{2,1,0:T(8,128)(2,1)S(1)}, u32[]{:S(2)}, u32[]{:S(2)}) collective-permute-start(bf16[8,8,4224]{2,1,0:T(8,128)(2,1)S(1)} %collective-permute-done.16.refs_11_), channel_id=1, source_target_pairs={{0,12},{1,13},{2,14},{3,15},{4,8},{5,9},{6,10},{7,11},{8,4},{9,5},... | collective-permute-start | bytes 1622024 | tf_op jit(solution)/shard_map/ppermute | solution.py:158
  108.6 10.6 %collective-permute-start.14 = (bf16[8,8,4224]{2,1,0:T(8,128)(2,1)S(1)}, bf16[8,8,4224]{2,1,0:T(8,128)(2,1)S(1)}, u32[]{:S(2)}, u32[]{:S(2)}) collective-permute-start(bf16[8,8,4224]{2,1,0:T(8,128)(2,1)S(1)} %collective-permute-done.13.refs_10_), channel_id=1, source_target_pairs={{0,48},{1,49},{2,50},{3,51},{4,52},{5,53},{6,54},{7,55},{8,56},{9,... | collective-permute-start | bytes 1622024 | tf_op jit(solution)/shard_map/ppermute | solution.py:158
  110.2 10.6 %collective-permute-start.11 = (bf16[8,8,4224]{2,1,0:T(8,128)(2,1)S(1)}, bf16[8,8,4224]{2,1,0:T(8,128)(2,1)S(1)}, u32[]{:S(2)}, u32[]{:S(2)}) collective-permute-start(bf16[8,8,4224]{2,1,0:T(8,128)(2,1)S(1)} %collective-permute-done.10.refs_9_), channel_id=1, source_target_pairs={{0,3},{1,2},{2,1},{3,0},{4,7},{5,6},{6,5},{7,4},{8,11},{9,10},{10,... | collective-permute-start | bytes 1622024 | tf_op jit(solution)/shard_map/ppermute | solution.py:158

commit v2 on v1

--- a/solution.py
+++ b/solution.py
@@ -140,7 +140,7 @@
     for piece, (colour, bits) in zip(pieces, which):
         hop = {SHARD[(colour + i) % 3]: (bits >> i) & 1 for i in range(3)}
         for j in range(8):
-            zz = z ^ (far * hop[SHARD[0]]) ^ (near * (j & 1))
+            zz = z ^ (3 * hop[SHARD[0]]) ^ (j & 1)
             yy = y ^ (far * hop[SHARD[1]]) ^ (near * ((j >> 1) & 1))
             xx = x ^ (far * hop[SHARD[2]]) ^ (near * ((j >> 2) & 1))
             away = (zz >> 1) ^ p
@@ -186,7 +186,7 @@
         pairs = []
         for q, z, y, x in everyone():
             m = near_mask(q)
-            pairs.append((flat(q, z, y, x), flat(q, z ^ (m * (j & 1)), y ^ (m * ((j >> 1) & 1)), x ^ (m * (j >> 2)))))
+            pairs.append((flat(q, z, y, x), flat(q, z ^ (j & 1), y ^ (m * ((j >> 1) & 1)), x ^ (m * (j >> 2)))))
         blocks.append(permute(block, pairs))
     whole = jnp.stack(blocks)
     third = rows // 3
@@ -194,7 +194,7 @@
     def swap(value, axis):
         pairs = []
         for q, z, y, x in everyone():
-            n = [far_mask(q) if axis == i else 0 for i in range(3)]
+            n = [(3 if i == 0 else far_mask(q)) if axis == i else 0 for i in range(3)]
             pairs.append((flat(q, z, y, x), flat(q, z ^ n[0], y ^ n[1], x ^ n[2])))
         return permute(value, pairs)
 

time: 122 us -> 152 us (1.25)
  the two profiles are of different devices: /device:TPU:0 before, /device:TPU:1 now
where the time goes in v2:
time: 152 us; the launch traced here: 150 us
  waiting for transfers between devices  97.1 us (64%)
  starting transfers between devices  39.5 us (26%)
  Pallas kernels  11.1 us (7%)
  between operations  2.06 us (1%)
    ppermute x30, waiting for transfers between devices, permute(): return lax.ppermute(value, AXES, pairs)  88.9 us
    ppermute x30, starting transfers between devices, permute(): return lax.ppermute(value, AXES, pairs)  28 us
    all_to_all x1, starting transfers between devices, per_device(): sums = lax.all_to_all(own, AXES, 0, 0, tiled=True)  11.5 us
    all_to_all x1, waiting for transfers between devices, per_device(): sums = lax.all_to_all(own, AXES, 0, 0, tiled=True)  8.17 us
    pallas_call x3, Pallas kernels, per_device(): pl.pallas_call(functools.partial(place_kernel, which), in_specs=[anywhere...  6.56 us
  transfers between devices with their start and end apart: 31, of which 16 were waited for; matrix products, arithmetic and copies ran while one was open for 0% of the time, Pallas kernels for 4%

profile of v2, /device:TPU:1, one launch (start us, length us, event | category | flops | bytes accessed | tf_op | source)
XLA Modules:
  0.0 150.1 jit_solution(14844804630600601544)
XLA Ops:
  0.6 1.7 %shard_map.101 = f32[128,128]{1,0:T(8,128)} custom-call(f32[48,2048]{1,0:T(8,128)} %gradient_ref.3), custom_call_target="tpu_custom_call" | custom-call | tf_op jit(solution)/shard_map/pallas_call | solution.py:218
  2.3 11.5 %all-to-all-start = ((f32[128,1,128]{2,1,0:T(1,128)}), f32[128,1,128]{2,1,0:T(1,128)S(1)}, u32[]{:S(2)}, u32[]{:S(2)}) async-start(f32[128,1,128]{2,1,0:T(1,128)} %bitcast.1), calls=%async_computation | async-start | bytes 131072 | tf_op jit(solution)/shard_map/all_to_all | solution.py:225
  15.1 8.2 %all-to-all-done = f32[128,1,128]{2,1,0:T(1,128)S(1)} async-done(((f32[128,1,128]{2,1,0:T(1,128)}), f32[128,1,128]{2,1,0:T(1,128)S(1)}, u32[]{:S(2)}, u32[]{:S(2)}) %all-to-all-start) | async-done | bytes 65568 | tf_op jit(solution)/shard_map/all_to_all | solution.py:225
  23.3 2.9 %shard_map.102 = (f32[48,2048]{1,0:T(8,128)}, f32[48,2048]{1,0:T(8,128)}, f32[48,2048]{1,0:T(8,128)}, bf16[24,2176]{1,0:T(8,128)(2,1)S(1)}, bf16[24,2176]{1,0:T(8,128)(2,1)S(1)}, /*index=5*/bf16[24,2176]{1,0:T(8,128)(2,1)S(1)}) custom-call(f32[1]{0:T(128)S(6)} %copy.27.max_norm_ref, s32[1]{0:T(128)S(6)} %copy.28.step_ref, f32[128,128]{1,0:T(8,128)S(1)} %bitcast.22, ...), custom_call_target="tpu_custom_call" | custom-call | tf_op jit(solution)/shard_map/pallas_call | solution.py:228
  26.2 0.7 collective-permute-start
  26.9 2.4 %collective-permute-start.1 = (bf16[24,2176]{1,0:T(8,128)(2,1)S(1)}, bf16[24,2176]{1,0:T(8,128)(2,1)S(1)}, u32[]{:S(2)}, u32[]{:S(2)}) collective-permute-start(bf16[24,2176]{1,0:T(8,128)(2,1)S(1)} %get-tuple-element.22), channel_id=1, source_target_pairs={{32,80},{33,81},{34,82},{35,83},{36,84},{37,85},{38,86},{39,87},{4... | collective-permute-start | bytes 313352 | tf_op jit(solution)/shard_map/ppermute | solution.py:158
  29.3 1.6 %collective-permute-done.one_ref = bf16[24,2176]{1,0:T(8,128)(2,1)S(1)} collective-permute-done((bf16[24,2176]{1,0:T(8,128)(2,1)S(1)}, bf16[24,2176]{1,0:T(8,128)(2,1)S(1)}, u32[]{:S(2)}, u32[]{:S(2)}) %collective-permute-start) | collective-permute-done | bytes 104480 | tf_op jit(solution)/shard_map/ppermute | solution.py:158
  30.9 3.2 %collective-permute-done.1.two_ref = bf16[24,2176]{1,0:T(8,128)(2,1)S(1)} collective-permute-done((bf16[24,2176]{1,0:T(8,128)(2,1)S(1)}, bf16[24,2176]{1,0:T(8,128)(2,1)S(1)}, u32[]{:S(2)}, u32[]{:S(2)}) %collective-permute-start.1) | collective-permute-done | bytes 104480 | tf_op jit(solution)/shard_map/ppermute | solution.py:158
  34.1 0.3 collective-permute-start.8
  34.5 3.4 %collective-permute-start.7 = (bf16[24,4224]{1,0:T(8,128)(2,1)S(1)}, bf16[24,4224]{1,0:T(8,128)(2,1)S(1)}, u32[]{:S(2)}, u32[]{:S(2)}) collective-permute-start(bf16[24,4224]{1,0:T(8,128)(2,1)S(1)} %shard_map.103), channel_id=1, source_target_pairs={{0,5},{1,4},{2,7},{3,6},{4,1},{5,0},{6,3},{7,2},{8,13},{9,12},{10,... | collective-permute-start | bytes 608264 | tf_op jit(solution)/shard_map/ppermute | solution.py:158
  37.9 3.0 %collective-permute-start.6 = (bf16[24,4224]{1,0:T(8,128)(2,1)S(1)}, bf16[24,4224]{1,0:T(8,128)(2,1)S(1)}, u32[]{:S(2)}, u32[]{:S(2)}) collective-permute-start(bf16[24,4224]{1,0:T(8,128)(2,1)S(1)} %shard_map.103), channel_id=1, source_target_pairs={{0,17},{1,16},{2,19},{3,18},{4,21},{5,20},{6,23},{7,22},{8,25},{9,... | collective-permute-start | bytes 608264 | tf_op jit(solution)/shard_map/ppermute | solution.py:158
  40.9 1.7 %collective-permute-start.5 = (bf16[24,4224]{1,0:T(8,128)(2,1)S(1)}, bf16[24,4224]{1,0:T(8,128)(2,1)S(1)}, u32[]{:S(2)}, u32[]{:S(2)}) collective-permute-start(bf16[24,4224]{1,0:T(8,128)(2,1)S(1)} %shard_map.103), channel_id=1, source_target_pairs={{0,1},{1,0},{2,3},{3,2},{4,5},{5,4},{6,7},{7,6},{8,9},{9,8},{10,11... | collective-permute-start | bytes 608264 | tf_op jit(solution)/shard_map/ppermute | solution.py:158
  42.6 0.0 collective-permute-start.2
  42.6 6.6 %collective-permute-done.2 = bf16[24,4224]{1,0:T(8,128)(2,1)S(1)} collective-permute-done((bf16[24,4224]{1,0:T(8,128)(2,1)S(1)}, bf16[24,4224]{1,0:T(8,128)(2,1)S(1)}, u32[]{:S(2)}, u32[]{:S(2)}) %collective-permute-start.2) | collective-permute-done | bytes 202784 | tf_op jit(solution)/shard_map/ppermute | solution.py:158
  49.2 1.0 collective-permute-start.3
  50.2 4.8 %collective-permute-done.3 = bf16[24,4224]{1,0:T(8,128)(2,1)S(1)} collective-permute-done((bf16[24,4224]{1,0:T(8,128)(2,1)S(1)}, bf16[24,4224]{1,0:T(8,128)(2,1)S(1)}, u32[]{:S(2)}, u32[]{:S(2)}) %collective-permute-start.3) | collective-permute-done | bytes 202784 | tf_op jit(solution)/shard_map/ppermute | solution.py:158
  55.0 0.9 collective-permute-start.4
  55.9 6.6 %collective-permute-done.4 = bf16[24,4224]{1,0:T(8,128)(2,1)S(1)} collective-permute-done((bf16[24,4224]{1,0:T(8,128)(2,1)S(1)}, bf16[24,4224]{1,0:T(8,128)(2,1)S(1)}, u32[]{:S(2)}, u32[]{:S(2)}) %collective-permute-start.4) | collective-permute-done | bytes 202784 | tf_op jit(solution)/shard_map/ppermute | solution.py:158
  62.6 0.0 collective-permute-done.5
  62.7 0.0 collective-permute-done.7
  62.7 0.1 fusion
  62.9 2.1 %collective-permute-start.28 = (bf16[8,8,4224]{2,1,0:T(8,128)(2,1)S(1)}, bf16[8,8,4224]{2,1,0:T(8,128)(2,1)S(1)}, u32[]{:S(2)}, u32[]{:S(2)}) collective-permute-start(bf16[8,8,4224]{2,1,0:T(8,128)(2,1)S(1)} %get-tuple-element.29.refs_2_), channel_id=1, source_target_pairs={{0,48},{1,49},{2,50},{3,51},{4,52},{5,53},{6,54},{7,55},{8,56},{9,... | collective-permute-start | bytes 1622024 | tf_op jit(solution)/shard_map/ppermute | solution.py:158
  65.0 1.5 collective-permute-start.26
  66.5 0.6 collective-permute-start.19
  67.1 10.8 %collective-permute-done.28.refs_8_ = bf16[8,8,4224]{2,1,0:T(8,128)(2,1)S(1)} collective-permute-done((bf16[8,8,4224]{2,1,0:T(8,128)(2,1)S(1)}, bf16[8,8,4224]{2,1,0:T(8,128)(2,1)S(1)}, u32[]{:S(2)}, u32[]{:S(2)}) %collective-permute-start.28) | collective-permute-done | bytes 540704 | tf_op jit(solution)/shard_map/ppermute | solution.py:158
  77.9 1.5 collective-permute-start.24
  79.4 0.6 collective-permute-start.18
  79.9 0.7 collective-permute-start.9
  80.7 8.8 %collective-permute-done.19.refs_1_ = bf16[8,8,4224]{2,1,0:T(8,128)(2,1)S(1)} collective-permute-done((bf16[8,8,4224]{2,1,0:T(8,128)(2,1)S(1)}, bf16[8,8,4224]{2,1,0:T(8,128)(2,1)S(1)}, u32[]{:S(2)}, u32[]{:S(2)}) %collective-permute-start.19) | collective-permute-done | bytes 540704 | tf_op jit(solution)/shard_map/ppermute | solution.py:158
  89.5 1.5 collective-permute-start.23
  91.0 1.2 collective-permute-done.24.refs_6_
  92.2 1.2 collective-permute-start.16
  93.4 1.5 %collective-permute-start.27 = (bf16[8,8,4224]{2,1,0:T(8,128)(2,1)S(1)}, bf16[8,8,4224]{2,1,0:T(8,128)(2,1)S(1)}, u32[]{:S(2)}, u32[]{:S(2)}) collective-permute-start(bf16[8,8,4224]{2,1,0:T(8,128)(2,1)S(1)} %collective-permute-done.26.refs_7_), channel_id=1, source_target_pairs={{0,48},{1,49},{2,50},{3,51},{4,52},{5,53},{6,54},{7,55},{8,56},{9,... | collective-permute-start | bytes 1622024 | tf_op jit(solution)/shard_map/ppermute | solution.py:158
  94.9 6.2 %collective-permute-done.9.refs_3_ = bf16[8,8,4224]{2,1,0:T(8,128)(2,1)S(1)} collective-permute-done((bf16[8,8,4224]{2,1,0:T(8,128)(2,1)S(1)}, bf16[8,8,4224]{2,1,0:T(8,128)(2,1)S(1)}, u32[]{:S(2)}, u32[]{:S(2)}) %collective-permute-start.9) | collective-permute-done | bytes 540704 | tf_op jit(solution)/shard_map/ppermute | solution.py:158
  101.1 1.2 collective-permute-start.22
  102.3 1.5 %collective-permute-done.23.refs_5_ = bf16[8,8,4224]{2,1,0:T(8,128)(2,1)S(1)} collective-permute-done((bf16[8,8,4224]{2,1,0:T(8,128)(2,1)S(1)}, bf16[8,8,4224]{2,1,0:T(8,128)(2,1)S(1)}, u32[]{:S(2)}, u32[]{:S(2)}) %collective-permute-start.23) | collective-permute-done | bytes 540704 | tf_op jit(solution)/shard_map/ppermute | solution.py:158
  103.8 0.0 collective-permute-start.10
  103.8 8.9 %collective-permute-done.16.refs_11_ = bf16[8,8,4224]{2,1,0:T(8,128)(2,1)S(1)} collective-permute-done((bf16[8,8,4224]{2,1,0:T(8,128)(2,1)S(1)}, bf16[8,8,4224]{2,1,0:T(8,128)(2,1)S(1)}, u32[]{:S(2)}, u32[]{:S(2)}) %collective-permute-start.16) | collective-permute-done | bytes 540704 | tf_op jit(solution)/shard_map/ppermute | solution.py:158
  112.7 0.6 collective-permute-start.25
  113.2 11.0 %collective-permute-done.27.refs_7_ = bf16[8,8,4224]{2,1,0:T(8,128)(2,1)S(1)} collective-permute-done((bf16[8,8,4224]{2,1,0:T(8,128)(2,1)S(1)}, bf16[8,8,4224]{2,1,0:T(8,128)(2,1)S(1)}, u32[]{:S(2)}, u32[]{:S(2)}) %collective-permute-start.27) | collective-permute-done | bytes 540704 | tf_op jit(solution)/shard_map/ppermute | solution.py:158
  124.3 0.6 collective-permute-start.21
  124.8 11.0 %collective-permute-done.22.refs_4_ = bf16[8,8,4224]{2,1,0:T(8,128)(2,1)S(1)} collective-permute-done((bf16[8,8,4224]{2,1,0:T(8,128)(2,1)S(1)}, bf16[8,8,4224]{2,1,0:T(8,128)(2,1)S(1)}, u32[]{:S(2)}, u32[]{:S(2)}) %collective-permute-start.22) | collective-permute-done | bytes 540704 | tf_op jit(solution)/shard_map/ppermute | solution.py:158
  135.9 1.2 collective-permute-start.14
  137.0 2.9 %shard_map.104 = (bf16[192,8,4096]{2,1,0:T(8,128)(2,1)}, bf16[192,8,128]{2,1,0:T(8,128)(2,1)}) custom-call(bf16[8,8,4224]{2,1,0:T(8,128)(2,1)S(1)} %get-tuple-element.31.refs_0_, bf16[8,8,4224]{2,1,0:T(8,128)(2,1)S(1)} %get-tuple-element.30.refs_1_, bf16[8,8,4224]{2,1,0:T(8,128)(2,1)S(1)} %get-tuple-element.29.refs_2_, ...), custom_call_target="tpu_custom_call" | custom-call | tf_op jit(solution)/shard_map/pallas_call | solution.py:241
  140.0 2.4 %shard_map.105 = (bf16[192,8,4096]{2,1,0:T(8,128)(2,1)}, bf16[192,8,128]{2,1,0:T(8,128)(2,1)}) custom-call(bf16[8,8,4224]{2,1,0:T(8,128)(2,1)S(1)} %collective-permute-done.18.refs_0_, bf16[8,8,4224]{2,1,0:T(8,128)(2,1)S(1)} %collective-permute-done.19.refs_1_, ...), custom_call_target="tpu_custom_call", output_to_operand_aliasing={{0}: (9, {}), {1}: (10, {})} | custom-call | tf_op jit(solution)/shard_map/pallas_call | solution.py:241
  142.4 1.9 %collective-permute-done.17.refs_2_ = bf16[8,8,4224]{2,1,0:T(8,128)(2,1)S(1)} collective-permute-done((bf16[8,8,4224]{2,1,0:T(8,128)(2,1)S(1)}, bf16[8,8,4224]{2,1,0:T(8,128)(2,1)S(1)}, u32[]{:S(2)}, u32[]{:S(2)}) %collective-permute-start.17) | collective-permute-done | bytes 540704 | tf_op jit(solution)/shard_map/ppermute | solution.py:158
  144.4 4.5 %collective-permute-done.14.refs_1_ = bf16[8,8,4224]{2,1,0:T(8,128)(2,1)S(1)} collective-permute-done((bf16[8,8,4224]{2,1,0:T(8,128)(2,1)S(1)}, bf16[8,8,4224]{2,1,0:T(8,128)(2,1)S(1)}, u32[]{:S(2)}, u32[]{:S(2)}) %collective-permute-start.14) | collective-permute-done | bytes 540704 | tf_op jit(solution)/shard_map/ppermute | solution.py:158
  148.9 1.2 shard_map.106
  (29 shorter events, 0.2 us)
Async XLA Ops:
  2.3 21.0 %all-to-all-start = ((f32[128,1,128]{2,1,0:T(1,128)}), f32[128,1,128]{2,1,0:T(1,128)S(1)}, u32[]{:S(2)}, u32[]{:S(2)}) async-start(f32[128,1,128]{2,1,0:T(1,128)} %bitcast.1), calls=%async_computation | async-start | bytes 131072 | tf_op jit(solution)/shard_map/all_to_all | solution.py:225
  26.2 4.7 %collective-permute-start = (bf16[24,2176]{1,0:T(8,128)(2,1)S(1)}, bf16[24,2176]{1,0:T(8,128)(2,1)S(1)}, u32[]{:S(2)}, u32[]{:S(2)}) collective-permute-start(bf16[24,2176]{1,0:T(8,128)(2,1)S(1)} %get-tuple-element.21), channel_id=1, source_target_pairs={{0,48},{1,49},{2,50},{3,51},{4,52},{5,53},{6,54},{7,55},{8,56},{9,... | collective-permute-start | bytes 313352 | tf_op jit(solution)/shard_map/ppermute | solution.py:158
  26.9 7.2 %collective-permute-start.1 = (bf16[24,2176]{1,0:T(8,128)(2,1)S(1)}, bf16[24,2176]{1,0:T(8,128)(2,1)S(1)}, u32[]{:S(2)}, u32[]{:S(2)}) collective-permute-start(bf16[24,2176]{1,0:T(8,128)(2,1)S(1)} %get-tuple-element.22), channel_id=1, source_target_pairs={{32,80},{33,81},{34,82},{35,83},{36,84},{37,85},{38,86},{39,87},{4... | collective-permute-start | bytes 313352 | tf_op jit(solution)/shard_map/ppermute | solution.py:158
  34.1 28.6 %collective-permute-start.8 = (bf16[24,4224]{1,0:T(8,128)(2,1)S(1)}, bf16[24,4224]{1,0:T(8,128)(2,1)S(1)}, u32[]{:S(2)}, u32[]{:S(2)}) collective-permute-start(bf16[24,4224]{1,0:T(8,128)(2,1)S(1)} %shard_map.103), channel_id=1, source_target_pairs={{0,21},{1,20},{2,23},{3,22},{4,17},{5,16},{6,19},{7,18},{8,29},{9,... | collective-permute-start | bytes 608264 | tf_op jit(solution)/shard_map/ppermute | solution.py:158
  34.5 28.2 %collective-permute-start.7 = (bf16[24,4224]{1,0:T(8,128)(2,1)S(1)}, bf16[24,4224]{1,0:T(8,128)(2,1)S(1)}, u32[]{:S(2)}, u32[]{:S(2)}) collective-permute-start(bf16[24,4224]{1,0:T(8,128)(2,1)S(1)} %shard_map.103), channel_id=1, source_target_pairs={{0,5},{1,4},{2,7},{3,6},{4,1},{5,0},{6,3},{7,2},{8,13},{9,12},{10,... | collective-permute-start | bytes 608264 | tf_op jit(solution)/shard_map/ppermute | solution.py:158
  37.9 24.8 %collective-permute-start.6 = (bf16[24,4224]{1,0:T(8,128)(2,1)S(1)}, bf16[24,4224]{1,0:T(8,128)(2,1)S(1)}, u32[]{:S(2)}, u32[]{:S(2)}) collective-permute-start(bf16[24,4224]{1,0:T(8,128)(2,1)S(1)} %shard_map.103), channel_id=1, source_target_pairs={{0,17},{1,16},{2,19},{3,18},{4,21},{5,20},{6,23},{7,22},{8,25},{9,... | collective-permute-start | bytes 608264 | tf_op jit(solution)/shard_map/ppermute | solution.py:158
  40.9 21.7 %collective-permute-start.5 = (bf16[24,4224]{1,0:T(8,128)(2,1)S(1)}, bf16[24,4224]{1,0:T(8,128)(2,1)S(1)}, u32[]{:S(2)}, u32[]{:S(2)}) collective-permute-start(bf16[24,4224]{1,0:T(8,128)(2,1)S(1)} %shard_map.103), channel_id=1, source_target_pairs={{0,1},{1,0},{2,3},{3,2},{4,5},{5,4},{6,7},{7,6},{8,9},{9,8},{10,11... | collective-permute-start | bytes 608264 | tf_op jit(solution)/shard_map/ppermute | solution.py:158
  42.6 6.7 %collective-permute-start.2 = (bf16[24,4224]{1,0:T(8,128)(2,1)S(1)}, bf16[24,4224]{1,0:T(8,128)(2,1)S(1)}, u32[]{:S(2)}, u32[]{:S(2)}) collective-permute-start(bf16[24,4224]{1,0:T(8,128)(2,1)S(1)} %shard_map.103), channel_id=1, source_target_pairs={{0,16},{1,17},{2,18},{3,19},{4,20},{5,21},{6,22},{7,23},{8,24},{9,... | collective-permute-start | bytes 608264 | tf_op jit(solution)/shard_map/ppermute | solution.py:158
  49.2 5.8 %collective-permute-start.3 = (bf16[24,4224]{1,0:T(8,128)(2,1)S(1)}, bf16[24,4224]{1,0:T(8,128)(2,1)S(1)}, u32[]{:S(2)}, u32[]{:S(2)}) collective-permute-start(bf16[24,4224]{1,0:T(8,128)(2,1)S(1)} %shard_map.103), channel_id=1, source_target_pairs={{0,4},{1,5},{2,6},{3,7},{4,0},{5,1},{6,2},{7,3},{8,12},{9,13},{10,... | collective-permute-start | bytes 608264 | tf_op jit(solution)/shard_map/ppermute | solution.py:158
  55.0 7.5 %collective-permute-start.4 = (bf16[24,4224]{1,0:T(8,128)(2,1)S(1)}, bf16[24,4224]{1,0:T(8,128)(2,1)S(1)}, u32[]{:S(2)}, u32[]{:S(2)}) collective-permute-start(bf16[24,4224]{1,0:T(8,128)(2,1)S(1)} %shard_map.103), channel_id=1, source_target_pairs={{0,20},{1,21},{2,22},{3,23},{4,16},{5,17},{6,18},{7,19},{8,28},{9,... | collective-permute-start | bytes 608264 | tf_op jit(solution)/shard_map/ppermute | solution.py:158
  62.9 15.1 %collective-permute-start.28 = (bf16[8,8,4224]{2,1,0:T(8,128)(2,1)S(1)}, bf16[8,8,4224]{2,1,0:T(8,128)(2,1)S(1)}, u32[]{:S(2)}, u32[]{:S(2)}) collective-permute-start(bf16[8,8,4224]{2,1,0:T(8,128)(2,1)S(1)} %get-tuple-element.29.refs_2_), channel_id=1, source_target_pairs={{0,48},{1,49},{2,50},{3,51},{4,52},{5,53},{6,54},{7,55},{8,56},{9,... | collective-permute-start | bytes 1622024 | tf_op jit(solution)/shard_map/ppermute | solution.py:158
  65.0 12.9 %collective-permute-start.20 = (bf16[8,8,4224]{2,1,0:T(8,128)(2,1)S(1)}, bf16[8,8,4224]{2,1,0:T(8,128)(2,1)S(1)}, u32[]{:S(2)}, u32[]{:S(2)}) collective-permute-start(bf16[8,8,4224]{2,1,0:T(8,128)(2,1)S(1)} %get-tuple-element.29.refs_2_), channel_id=1, source_target_pairs={{0,12},{1,13},{2,14},{3,15},{4,8},{5,9},{6,10},{7,11},{8,4},{9,5},... | collective-permute-start | bytes 1622024 | tf_op jit(solution)/shard_map/ppermute | solution.py:158
  65.0 14.4 %collective-permute-start.15 = (bf16[8,8,4224]{2,1,0:T(8,128)(2,1)S(1)}, bf16[8,8,4224]{2,1,0:T(8,128)(2,1)S(1)}, u32[]{:S(2)}, u32[]{:S(2)}) collective-permute-start(bf16[8,8,4224]{2,1,0:T(8,128)(2,1)S(1)} %get-tuple-element.29.refs_2_), channel_id=1, source_target_pairs={{0,3},{1,2},{2,1},{3,0},{4,7},{5,6},{6,5},{7,4},{8,11},{9,10},{10,... | collective-permute-start | bytes 1622024 | tf_op jit(solution)/shard_map/ppermute | solution.py:158
  65.0 14.9 %collective-permute-start.26 = (bf16[8,8,4224]{2,1,0:T(8,128)(2,1)S(1)}, bf16[8,8,4224]{2,1,0:T(8,128)(2,1)S(1)}, u32[]{:S(2)}, u32[]{:S(2)}) collective-permute-start(bf16[8,8,4224]{2,1,0:T(8,128)(2,1)S(1)} %get-tuple-element.30.refs_1_), channel_id=1, source_target_pairs={{0,3},{1,2},{2,1},{3,0},{4,7},{5,6},{6,5},{7,4},{8,11},{9,10},{10,... | collective-permute-start | bytes 1622024 | tf_op jit(solution)/shard_map/ppermute | solution.py:158
  66.5 23.0 %collective-permute-start.19 = (bf16[8,8,4224]{2,1,0:T(8,128)(2,1)S(1)}, bf16[8,8,4224]{2,1,0:T(8,128)(2,1)S(1)}, u32[]{:S(2)}, u32[]{:S(2)}) collective-permute-start(bf16[8,8,4224]{2,1,0:T(8,128)(2,1)S(1)} %get-tuple-element.30.refs_1_), channel_id=1, source_target_pairs={{0,48},{1,49},{2,50},{3,51},{4,52},{5,53},{6,54},{7,55},{8,56},{9,... | collective-permute-start | bytes 1622024 | tf_op jit(solution)/shard_map/ppermute | solution.py:158
  77.9 11.6 %collective-permute-start.12 = (bf16[8,8,4224]{2,1,0:T(8,128)(2,1)S(1)}, bf16[8,8,4224]{2,1,0:T(8,128)(2,1)S(1)}, u32[]{:S(2)}, u32[]{:S(2)}) collective-permute-start(bf16[8,8,4224]{2,1,0:T(8,128)(2,1)S(1)} %get-tuple-element.30.refs_1_), channel_id=1, source_target_pairs={{0,12},{1,13},{2,14},{3,15},{4,8},{5,9},{6,10},{7,11},{8,4},{9,5},... | collective-permute-start | bytes 1622024 | tf_op jit(solution)/shard_map/ppermute | solution.py:158
  77.9 14.3 %collective-permute-start.24 = (bf16[8,8,4224]{2,1,0:T(8,128)(2,1)S(1)}, bf16[8,8,4224]{2,1,0:T(8,128)(2,1)S(1)}, u32[]{:S(2)}, u32[]{:S(2)}) collective-permute-start(bf16[8,8,4224]{2,1,0:T(8,128)(2,1)S(1)} %get-tuple-element.31.refs_0_), channel_id=1, source_target_pairs={{0,12},{1,13},{2,14},{3,15},{4,8},{5,9},{6,10},{7,11},{8,4},{9,5},... | collective-permute-start | bytes 1622024 | tf_op jit(solution)/shard_map/ppermute | solution.py:158
  79.4 14.0 %collective-permute-start.18 = (bf16[8,8,4224]{2,1,0:T(8,128)(2,1)S(1)}, bf16[8,8,4224]{2,1,0:T(8,128)(2,1)S(1)}, u32[]{:S(2)}, u32[]{:S(2)}) collective-permute-start(bf16[8,8,4224]{2,1,0:T(8,128)(2,1)S(1)} %get-tuple-element.31.refs_0_), channel_id=1, source_target_pairs={{0,3},{1,2},{2,1},{3,0},{4,7},{5,6},{6,5},{7,4},{8,11},{9,10},{10,... | collective-permute-start | bytes 1622024 | tf_op jit(solution)/shard_map/ppermute | solution.py:158
  79.9 21.1 %collective-permute-start.9 = (bf16[8,8,4224]{2,1,0:T(8,128)(2,1)S(1)}, bf16[8,8,4224]{2,1,0:T(8,128)(2,1)S(1)}, u32[]{:S(2)}, u32[]{:S(2)}) collective-permute-start(bf16[8,8,4224]{2,1,0:T(8,128)(2,1)S(1)} %get-tuple-element.31.refs_0_), channel_id=1, source_target_pairs={{0,48},{1,49},{2,50},{3,51},{4,52},{5,53},{6,54},{7,55},{8,56},{9,... | collective-permute-start | bytes 1622024 | tf_op jit(solution)/shard_map/ppermute | solution.py:158
  89.5 12.8 %collective-permute-start.29 = (bf16[8,8,4224]{2,1,0:T(8,128)(2,1)S(1)}, bf16[8,8,4224]{2,1,0:T(8,128)(2,1)S(1)}, u32[]{:S(2)}, u32[]{:S(2)}) collective-permute-start(bf16[8,8,4224]{2,1,0:T(8,128)(2,1)S(1)} %collective-permute-done.28.refs_8_), channel_id=1, source_target_pairs={{0,12},{1,13},{2,14},{3,15},{4,8},{5,9},{6,10},{7,11},{8,4},{9,5},... | collective-permute-start | bytes 1622024 | tf_op jit(solution)/shard_map/ppermute | solution.py:158
  89.5 14.3 %collective-permute-start.23 = (bf16[8,8,4224]{2,1,0:T(8,128)(2,1)S(1)}, bf16[8,8,4224]{2,1,0:T(8,128)(2,1)S(1)}, u32[]{:S(2)}, u32[]{:S(2)}) collective-permute-start(bf16[8,8,4224]{2,1,0:T(8,128)(2,1)S(1)} %collective-permute-done.15.refs_5_), channel_id=1, source_target_pairs={{0,12},{1,13},{2,14},{3,15},{4,8},{5,9},{6,10},{7,11},{8,4},{9,5},... | collective-permute-start | bytes 1622024 | tf_op jit(solution)/shard_map/ppermute | solution.py:158
  92.2 20.5 %collective-permute-start.16 = (bf16[8,8,4224]{2,1,0:T(8,128)(2,1)S(1)}, bf16[8,8,4224]{2,1,0:T(8,128)(2,1)S(1)}, u32[]{:S(2)}, u32[]{:S(2)}) collective-permute-start(bf16[8,8,4224]{2,1,0:T(8,128)(2,1)S(1)} %collective-permute-done.15.refs_5_), channel_id=1, source_target_pairs={{0,48},{1,49},{2,50},{3,51},{4,52},{5,53},{6,54},{7,55},{8,56},{9,... | collective-permute-start | bytes 1622024 | tf_op jit(solution)/shard_map/ppermute | solution.py:158
  93.4 30.9 %collective-permute-start.27 = (bf16[8,8,4224]{2,1,0:T(8,128)(2,1)S(1)}, bf16[8,8,4224]{2,1,0:T(8,128)(2,1)S(1)}, u32[]{:S(2)}, u32[]{:S(2)}) collective-permute-start(bf16[8,8,4224]{2,1,0:T(8,128)(2,1)S(1)} %collective-permute-done.26.refs_7_), channel_id=1, source_target_pairs={{0,48},{1,49},{2,50},{3,51},{4,52},{5,53},{6,54},{7,55},{8,56},{9,... | collective-permute-start | bytes 1622024 | tf_op jit(solution)/shard_map/ppermute | solution.py:158
  101.1 34.8 %collective-permute-start.22 = (bf16[8,8,4224]{2,1,0:T(8,128)(2,1)S(1)}, bf16[8,8,4224]{2,1,0:T(8,128)(2,1)S(1)}, u32[]{:S(2)}, u32[]{:S(2)}) collective-permute-start(bf16[8,8,4224]{2,1,0:T(8,128)(2,1)S(1)} %collective-permute-done.12.refs_4_), channel_id=1, source_target_pairs={{0,48},{1,49},{2,50},{3,51},{4,52},{5,53},{6,54},{7,55},{8,56},{9,... | collective-permute-start | bytes 1622024 | tf_op jit(solution)/shard_map/ppermute | solution.py:158
  102.3 33.6 %collective-permute-start.13 = (bf16[8,8,4224]{2,1,0:T(8,128)(2,1)S(1)}, bf16[8,8,4224]{2,1,0:T(8,128)(2,1)S(1)}, u32[]{:S(2)}, u32[]{:S(2)}) collective-permute-start(bf16[8,8,4224]{2,1,0:T(8,128)(2,1)S(1)} %collective-permute-done.12.refs_4_), channel_id=1, source_target_pairs={{0,3},{1,2},{2,1},{3,0},{4,7},{5,6},{6,5},{7,4},{8,11},{9,10},{10,... | collective-permute-start | bytes 1622024 | tf_op jit(solution)/shard_map/ppermute | solution.py:158
  103.8 33.2 %collective-permute-start.10 = (bf16[8,8,4224]{2,1,0:T(8,128)(2,1)S(1)}, bf16[8,8,4224]{2,1,0:T(8,128)(2,1)S(1)}, u32[]{:S(2)}, u32[]{:S(2)}) collective-permute-start(bf16[8,8,4224]{2,1,0:T(8,128)(2,1)S(1)} %collective-permute-done.9.refs_3_), channel_id=1, source_target_pairs={{0,12},{1,13},{2,14},{3,15},{4,8},{5,9},{6,10},{7,11},{8,4},{9,5},... | collective-permute-start | bytes 1622024 | tf_op jit(solution)/shard_map/ppermute | solution.py:158
  112.7 27.3 %collective-permute-start.25 = (bf16[8,8,4224]{2,1,0:T(8,128)(2,1)S(1)}, bf16[8,8,4224]{2,1,0:T(8,128)(2,1)S(1)}, u32[]{:S(2)}, u32[]{:S(2)}) collective-permute-start(bf16[8,8,4224]{2,1,0:T(8,128)(2,1)S(1)} %collective-permute-done.24.refs_6_), channel_id=1, source_target_pairs={{0,3},{1,2},{2,1},{3,0},{4,7},{5,6},{6,5},{7,4},{8,11},{9,10},{10,... | collective-permute-start | bytes 1622024 | tf_op jit(solution)/shard_map/ppermute | solution.py:158
  124.3 15.7 %collective-permute-start.21 = (bf16[8,8,4224]{2,1,0:T(8,128)(2,1)S(1)}, bf16[8,8,4224]{2,1,0:T(8,128)(2,1)S(1)}, u32[]{:S(2)}, u32[]{:S(2)}) collective-permute-start(bf16[8,8,4224]{2,1,0:T(8,128)(2,1)S(1)} %collective-permute-done.9.refs_3_), channel_id=1, source_target_pairs={{0,3},{1,2},{2,1},{3,0},{4,7},{5,6},{6,5},{7,4},{8,11},{9,10},{10,... | collective-permute-start | bytes 1622024 | tf_op jit(solution)/shard_map/ppermute | solution.py:158
  135.8 8.5 %collective-permute-start.17 = (bf16[8,8,4224]{2,1,0:T(8,128)(2,1)S(1)}, bf16[8,8,4224]{2,1,0:T(8,128)(2,1)S(1)}, u32[]{:S(2)}, u32[]{:S(2)}) collective-permute-start(bf16[8,8,4224]{2,1,0:T(8,128)(2,1)S(1)} %collective-permute-done.16.refs_11_), channel_id=1, source_target_pairs={{0,12},{1,13},{2,14},{3,15},{4,8},{5,9},{6,10},{7,11},{8,4},{9,5},... | collective-permute-start | bytes 1622024 | tf_op jit(solution)/shard_map/ppermute | solution.py:158
  135.9 13.0 %collective-permute-start.14 = (bf16[8,8,4224]{2,1,0:T(8,128)(2,1)S(1)}, bf16[8,8,4224]{2,1,0:T(8,128)(2,1)S(1)}, u32[]{:S(2)}, u32[]{:S(2)}) collective-permute-start(bf16[8,8,4224]{2,1,0:T(8,128)(2,1)S(1)} %collective-permute-done.13.refs_10_), channel_id=1, source_target_pairs={{0,48},{1,49},{2,50},{3,51},{4,52},{5,53},{6,54},{7,55},{8,56},{9,... | collective-permute-start | bytes 1622024 | tf_op jit(solution)/shard_map/ppermute | solution.py:158
  137.0 11.9 %collective-permute-start.11 = (bf16[8,8,4224]{2,1,0:T(8,128)(2,1)S(1)}, bf16[8,8,4224]{2,1,0:T(8,128)(2,1)S(1)}, u32[]{:S(2)}, u32[]{:S(2)}) collective-permute-start(bf16[8,8,4224]{2,1,0:T(8,128)(2,1)S(1)} %collective-permute-done.10.refs_9_), channel_id=1, source_target_pairs={{0,3},{1,2},{2,1},{3,0},{4,7},{5,6},{6,5},{7,4},{8,11},{9,10},{10,... | collective-permute-start | bytes 1622024 | tf_op jit(solution)/shard_map/ppermute | solution.py:158
